TPU v7x, 8 devices: a whole 2x2x1 slice. The times are simulated.
8 devices in a mesh: dp: 2 (over z, y), ep: 4 (over x, core).
Axes of the slice: x: 2, y: 2, z: 1, core: 2. Of those that a mesh axis runs over, the one named last changes fastest.
Arguments:
- x_a: bfloat16 [2048, 2304], P(('dp', 'ep')), parts along dimension 0
- route_a: int32 [2048, 2], P(('dp', 'ep')), parts along dimension 0
- gate_a: float32 [2048, 2], P(('dp', 'ep')), parts along dimension 0
- h_b: bfloat16 [2048, 2304], P(('dp', 'ep')), parts along dimension 0
- attn_b: bfloat16 [2048, 2304], P(('dp', 'ep')), parts along dimension 0
- route_b: int32 [2048, 2], P(('dp', 'ep')), parts along dimension 0
- gate_b: float32 [2048, 2], P(('dp', 'ep')), parts along dimension 0
- w_qkv: bfloat16 [2304, 6912], replicated
- w_o: bfloat16 [2304, 2304], replicated
- w_gate: bfloat16 [8, 2304, 5760], P('ep')
- w_up: bfloat16 [8, 2304, 5760], P('ep')
- w_down: bfloat16 [8, 5760, 2304], P('ep')
Outputs:
- output 1: bfloat16 [2048, 2304], P(('dp', 'ep')), parts along dimension 0
- output 2: bfloat16 [2048, 2304], P(('dp', 'ep')), parts along dimension 0
- output 3: bfloat16 [2048, 6912], P(('dp', 'ep')), parts along dimension 0
There are 2 independent parts. A program takes and returns all parts, laid end to end along the dimension named above; an argument that names none is the same for every part.
All inputs are finite; a program needn't handle non-finite values.
Results may differ from a plain program's by a relative error of at most 0.0121025.
Values are sent between devices in bfloat16 or wider.
A program may use at most 1 GiB of HBM per device.

v0:
```python
import functools

import jax
import jax.numpy as jnp
from jax import lax
from jax.experimental import pallas as pl
from jax.experimental.pallas import tpu as pltpu
from jax.sharding import PartitionSpec as P


BF16, F32, I32 = jnp.bfloat16, jnp.float32, jnp.int32
N_SRC = 4
SLOTS = 128
HALF = 512
VARIANTS = (256, 384, 512)
FC, DC = 640, 768
MIB = 2 ** 20

COL_POS, COL_BOTH, COL_OWN, COL_CNT, COL_TOP = 0, 16, 28, 31, 34


def swap(x, k):
    return lax.ppermute(x, 'ep', [(i, i ^ k) for i in range(N_SRC)])


def after(x, dep):
    return lax.optimization_barrier((x, dep))[0]


def route_kernel(me_ref, m0, m1, m2, m3, pos_ref, tab_ref, cnt_ref, mid_ref, top_ref):
    me = me_ref[0]
    n_tok = m0.shape[1]
    before = (lax.broadcasted_iota(I32, (n_tok, n_tok), 0)
              < lax.broadcasted_iota(I32, (n_tok, n_tok), 1)).astype(BF16)
    metas = [m[...] for m in (m0, m1, m2, m3)]
    for mb in range(2):
        r0 = [m[2 * mb:2 * mb + 1] for m in metas]
        r1 = [m[2 * mb + 1:2 * mb + 2] for m in metas]
        g0 = [m[4 + 2 * mb:5 + 2 * mb] for m in metas]
        g1 = [m[5 + 2 * mb:6 + 2 * mb] for m in metas]
        sel, gate = [], []
        for l in range(2):
            e = (2 * me + l).astype(F32)
            for s in range(N_SRC):
                h0 = (r0[s] == e).astype(F32)
                h1 = (r1[s] == e).astype(F32)
                sel.append(h0 + h1)
                gate.append(h0 * g0[s] + h1 * g1[s])
        both = []
        for s in range(N_SRC):
            b = sel[s] + sel[N_SRC + s] > 1.5
            both += [b.astype(F32), jnp.where(b, gate[s], 1.0), jnp.where(b, gate[N_SRC + s], 1.0)]
        sel = jnp.concatenate(sel, axis=0)
        rank = jnp.dot(sel.astype(BF16), before, preferred_element_type=F32)
        pos = jnp.where(sel > 0, rank, -1.0)
        pos_ref[mb] = pos
        cnt_ref[mb] = jnp.broadcast_to(jnp.sum(sel, axis=1, keepdims=True), cnt_ref.shape[1:]).astype(I32)

        def owners(s):
            counts, gates = [], []
            for k in range(N_SRC):
                lo = (2 * jnp.bitwise_xor(me, k)).astype(F32)
                o0 = jnp.logical_or(r0[s] == lo, r0[s] == lo + 1).astype(F32)
                o1 = jnp.logical_or(r1[s] == lo, r1[s] == lo + 1).astype(F32)
                counts.append(o0 + o1)
                gates.append(o0 * g0[s] + o1 * g1[s])
            return counts, gates

        def coefs(mix, gates):
            return [jnp.where(mix, 1.0, 0.0)] + [jnp.where(mix, g, 1.0) for g in gates]

        c, g = owners(0)
        c2, g2 = owners(2)
        rows = [pos] + gate + both
        rows += coefs(jnp.logical_and(c[0] == 1.0, c[1] == 1.0), g[:2])
        rows += coefs(jnp.logical_and(c2[0] == 1.0, c2[1] == 1.0), g2[:2])
        rows += coefs(c[0] + c[1] == 1.0, [g[0] + g[1], g[2] + g[3]])
        rows = jnp.concatenate(rows + [jnp.zeros((128 - COL_TOP - 3, n_tok), F32)], axis=0)
        t = rows.T
        tab_ref[mb] = t
        for ref, cols in ((mid_ref, range(COL_CNT, COL_CNT + 3)),
                          (top_ref, [*range(COL_OWN, COL_OWN + 3), *range(COL_TOP, COL_TOP + 3)])):
            for k, c in enumerate(cols):
                ref[len(cols) * mb + k] = jnp.broadcast_to(t[:, c:c + 1], (n_tok, 128))


def route(me, metas):
    n_tok = metas[0].shape[1]
    return pl.pallas_call(
        route_kernel,
        out_shape=[jax.ShapeDtypeStruct((2, 8, n_tok), F32), jax.ShapeDtypeStruct((2, n_tok, 128), F32),
                   jax.ShapeDtypeStruct((2, 8, 128), I32), jax.ShapeDtypeStruct((6, n_tok, 128), F32),
                   jax.ShapeDtypeStruct((12, n_tok, 128), F32)],
        in_specs=[pl.BlockSpec(memory_space=pltpu.SMEM)] + [pl.BlockSpec(memory_space=pltpu.VMEM)] * 4,
        out_specs=[pl.BlockSpec(memory_space=pltpu.VMEM)] * 5,
        name='route',
    )(me, *metas)


def offset(cnt, l, loc, k):
    off = 0
    for q in range(4 if not isinstance(k, int) else k):
        n = lax.div(cnt[q // 2, l * N_SRC + 2 * loc + q % 2, 0] + 15, 16) * 16
        off = off + (n if isinstance(k, int) else jnp.where(q < k, n, 0))
    return off


def for_rows(m, body):
    lo = 0
    for rows in VARIANTS:
        pl.when(jnp.logical_and(m > lo, m <= rows))(functools.partial(body, rows))
        lo = rows


def up_step(loc, i, n, nc, cnt, pos, us, wg, wu, x, w, sem, h, whole):
    ns = w.shape[0]

    def copies(j):
        l, c, s = lax.div(j, nc), lax.rem(j, nc), lax.rem(j, ns)
        cols = pl.ds(pl.multiple_of(c * FC, 128), FC)
        return [pltpu.make_async_copy(wg.at[l, :, cols], w.at[s, :, pl.ds(0, FC)], sem.at[s, 0]),
                pltpu.make_async_copy(wu.at[l, :, cols], w.at[s, :, pl.ds(FC, FC)], sem.at[s, 1])]

    @pl.when(i == 0)
    def _():
        for j in range(ns - 1):
            for c in copies(j):
                c.start()
        x[...] = jnp.zeros_like(x)
        for l in range(2):
            for k in range(4):
                q = l * N_SRC + 2 * loc + k % 2
                p = pos[k // 2, q:q + 1, :]
                pick = (lax.broadcasted_iota(I32, (SLOTS, p.shape[1]), 0).astype(F32) == p).astype(BF16)
                rows = jnp.dot(pick, us[k][...], preferred_element_type=F32)
                x[l, pl.ds(pl.multiple_of(offset(cnt, l, loc, k), 16), SLOTS), :] = rows.astype(BF16)

    @pl.when(i + ns - 1 < n)
    def _():
        for c in copies(i + ns - 1):
            c.start()

    @pl.when(i < n)
    def _():
        for c in copies(i):
            c.wait()
        l, s = lax.div(i, nc), lax.rem(i, ns)
        cols = pl.ds(pl.multiple_of(lax.rem(i, nc) * FC, 128), FC)

        def body(rows):
            r = jnp.dot(x[l, :rows], w[s], preferred_element_type=F32)
            res = (jax.nn.silu(r[:, :FC]) * r[:, FC:]).astype(BF16)
            if whole:
                h[l, :rows, cols] = res
            else:
                h[0, :rows] = res

        for_rows(offset(cnt, l, loc, 4), body)


def up_kernel(loc, nc, cnt, pos, ua0, ua1, ub0, ub1, wg, wu, h, x, w, sem):
    up_step(loc, pl.program_id(0), 2 * nc, nc, cnt, pos, (ua0, ua1, ub0, ub1), wg, wu, x, w, sem, h, False)


def up(loc, cnt, pos, us, wg, wu):
    d, ff = wg.shape[1:]
    ns = 3
    vmem, hbm = pl.BlockSpec(memory_space=pltpu.VMEM), pl.BlockSpec(memory_space=pl.ANY)
    flops = 4 * d * ff * 2 * HALF
    return pl.pallas_call(
        functools.partial(up_kernel, loc, ff // FC),
        out_shape=jax.ShapeDtypeStruct((2, HALF, ff), BF16),
        grid_spec=pltpu.PrefetchScalarGridSpec(
            num_scalar_prefetch=1, grid=(2 * (ff // FC),), in_specs=[vmem] * 5 + [hbm, hbm],
            out_specs=pl.BlockSpec((1, HALF, FC), lambda i, c: (lax.div(i, ff // FC), 0, lax.rem(i, ff // FC))),
            scratch_shapes=[pltpu.VMEM((2, HALF, d), BF16), pltpu.VMEM((ns, d, 2 * FC), BF16),
                            pltpu.SemaphoreType.DMA((ns, 2))]),
        compiler_params=pltpu.CompilerParams(vmem_limit_bytes=63 * MIB),
        cost_estimate=pl.CostEstimate(flops=flops, bytes_accessed=flops // 512, transcendentals=0),
    )(cnt, pos, *us, wg, wu)


def ffn_kernel(loc, n1, nc, cnt, tab, *refs):
    it = iter(refs)
    pos = next(it) if n1 else None
    us = [next(it) for _ in range(4)]
    wg, wu = (next(it), next(it)) if n1 else (None, None)
    h_in = None if n1 else next(it)
    wd, keep, send, h, y, w2, pick, coef, s2 = [next(it) for _ in range(9)]
    x, w1, s1 = [next(it) for _ in range(3)] if n1 else (None,) * 3
    sh = None if n1 else next(it)
    i = pl.program_id(0)
    n_tok = tab.shape[1]
    j = i - n1
    n2 = pl.num_programs(0) - n1

    def copy2(j):
        cols = pl.ds(pl.multiple_of(lax.div(j, 2) * DC, 128), DC)
        return pltpu.make_async_copy(wd.at[lax.rem(j, 2), :, cols], w2.at[lax.rem(j, 2)], s2.at[lax.rem(j, 2)])

    def h_copy(e, rows):
        return pltpu.make_async_copy(h_in.at[e, pl.ds(0, rows)], h.at[e, pl.ds(0, rows)], sh.at[e])

    def h_copies(e, act):
        for_rows(offset(cnt, e, loc, 4), lambda rows: act(h_copy(e, rows)))

    if not n1:
        @pl.when(i == 0)
        def _():
            h_copies(0, lambda c: c.start())
            copy2(0).start()

    @pl.when(i == 0)
    def _():
        y[...] = jnp.zeros_like(y)
        lane = lax.broadcasted_iota(I32, (n_tok, SLOTS), 1).astype(F32)
        for mb in range(2):
            t = tab[mb]
            for e in range(2):
                for par in range(2):
                    c = COL_POS + e * N_SRC + 2 * loc + par
                    pick[4 * mb + 2 * e + par] = (t[:, c:c + 1] == lane).astype(BF16)
            for par in range(2):
                for k in range(3):
                    c = COL_BOTH + 3 * (2 * loc + par) + k
                    coef[6 * mb + 3 * par + k] = jnp.broadcast_to(t[:, c:c + 1], (n_tok, 128))

    if n1:
        up_step(loc, i, n1, nc, cnt, pos, us, wg, wu, x, w1, s1, h, True)

        @pl.when(i == n1 - 2)
        def _():
            copy2(0).start()

    @pl.when(j >= 0)
    def _():
        l = lax.rem(j, 2)
        if not n1:
            @pl.when(j == 0)
            def _():
                h_copies(0, lambda c: c.wait())
                h_copies(1, lambda c: c.start())

            @pl.when(j == 1)
            def _():
                h_copies(1, lambda c: c.wait())

        @pl.when(j + 1 < n2)
        def _():
            copy2(j + 1).start()

        copy2(j).wait()

        def body(rows):
            y[l, :rows] = jnp.dot(h[l, :rows], w2[l], preferred_element_type=F32).astype(BF16)

        for_rows(offset(cnt, l, loc, 4), body)

        @pl.when(l == 1)
        def _():
            def part(mb, carry):
                for par, out in enumerate((keep, send)):
                    vals = []
                    for e in range(2):
                        r0 = pl.multiple_of(offset(cnt, e, loc, 2 * mb + par), 16)
                        vals.append(jnp.dot(pick[4 * mb + 2 * e + par], y[e, pl.ds(r0, SLOTS), :],
                                            preferred_element_type=F32))
                    a, c0, c1 = [coef[6 * mb + 3 * par + k] for k in range(3)]
                    u = us[par], us[2 + par]
                    for c in lanes(DC):
                        if n1:
                            cols = pl.ds(pl.multiple_of(lax.div(j, 2) * DC + c.start, 128), 128)
                        else:
                            cols = c
                        uc = jnp.where(mb == 0, u[0][:, cols], u[1][:, cols]).astype(F32)
                        mixed = c0 * vals[0][:, c] + c1 * vals[1][:, c]
                        out[pl.ds(pl.multiple_of(mb * n_tok, 256), n_tok), c] = (a * uc + mixed).astype(BF16)
                return carry

            lax.fori_loop(0, 2, part, 0)


def ffn(loc, cnt, tab, us, wd, *, pos=None, wg=None, wu=None, h_in=None):
    n_tok, d = us[0].shape
    ff = wd.shape[1]
    nc = ff // FC
    n1 = 2 * nc if h_in is None else 0
    ns1 = 2
    once = lambda a: pl.BlockSpec(a.shape, lambda i, c: (0,) * a.ndim, pipeline_mode=pl.Buffered(1))
    hbm = pl.BlockSpec(memory_space=pl.ANY)
    col = lambda i, c: (0, lax.div(jnp.maximum(i - n1, 0), 2))
    scratch = [pltpu.VMEM((2, HALF, ff), BF16), pltpu.VMEM((2, HALF, DC), BF16), pltpu.VMEM((2, ff, DC), BF16),
               pltpu.VMEM((8, n_tok, SLOTS), BF16), pltpu.VMEM((12, n_tok, 128), F32), pltpu.SemaphoreType.DMA((2,))]
    if n1:
        args = [tab, pos, *us, wg, wu, wd]
        specs = [once(tab), once(pos)] + [once(u) for u in us] + [hbm] * 3
        scratch += [pltpu.VMEM((2, HALF, d), BF16), pltpu.VMEM((ns1, d, 2 * FC), BF16), pltpu.SemaphoreType.DMA((ns1, 2))]
    else:
        args = [tab, *us, h_in, wd]
        specs = [once(tab)] + [pl.BlockSpec((n_tok, DC), col)] * 4 + [hbm] * 2
        scratch += [pltpu.SemaphoreType.DMA((2,))]
    out = jax.ShapeDtypeStruct((2 * n_tok, d), BF16)
    out_spec = pl.BlockSpec((2 * n_tok, DC), col)
    flops = (2 if h_in is not None else 6) * d * ff * 2 * HALF
    return pl.pallas_call(
        functools.partial(ffn_kernel, loc, n1, nc), out_shape=[out, out],
        grid_spec=pltpu.PrefetchScalarGridSpec(num_scalar_prefetch=1, grid=(n1 + 2 * (d // DC),), in_specs=specs,
                                               out_specs=[out_spec, out_spec], scratch_shapes=scratch),
        compiler_params=pltpu.CompilerParams(vmem_limit_bytes=67043328),
        cost_estimate=pl.CostEstimate(flops=flops, bytes_accessed=flops // 512, transcendentals=0),
    )(cnt, *args)


def lincomb(c, k, u, a, b):
    return (c[k] * u.astype(F32) + (c[k + 1] * a.astype(F32) + c[k + 2] * b.astype(F32))).astype(BF16)


def lanes(width):
    return [slice(c * 128, (c + 1) * 128) for c in range(width // 128)]


def there_kernel(coef, u0, u1, keep, got, out):
    n = u0.shape[0]
    for mb, u in enumerate((u0, u1)):
        r = slice(mb * n, (mb + 1) * n)
        for c in lanes(u.shape[1]):
            out[r, c] = lincomb(coef, 3 * mb, u[:, c], keep[r, c], got[r, c])


def top_kernel(coef, u0, u1, keep, got, back, *outs):
    n = u0.shape[0]
    for mb, u in enumerate((u0, u1)):
        r = slice(mb * n, (mb + 1) * n)
        for c in lanes(u.shape[1]):
            here = lincomb(coef, 6 * mb, u[:, c], keep[r, c], got[r, c])
            outs[mb][:, c] = lincomb(coef, 6 * mb + 3, u[:, c], here, back[r, c])


def mix(kernel, coef, us, rows, outs):
    n, d = us[0].shape
    bw = 768
    at = lambda r: pl.BlockSpec((r, bw), lambda i: (0, i))
    return pl.pallas_call(
        kernel, out_shape=[jax.ShapeDtypeStruct((r, d), BF16) for r in outs], grid=(d // bw,),
        in_specs=[pl.BlockSpec(coef.shape, lambda i: (0, 0, 0))] + [at(n)] * 2 + [at(2 * n)] * len(rows),
        out_specs=[at(r) for r in outs],
        cost_estimate=pl.CostEstimate(flops=10 ** 9, bytes_accessed=10 ** 6, transcendentals=0),
    )(coef, *us, *rows)


def dense_kernel(x, w, *refs):
    p = jnp.dot(x[...], w[...], preferred_element_type=F32).astype(BF16)
    if len(refs) > 1:
        p = (refs[0][...].astype(F32) + p.astype(F32)).astype(BF16)
    refs[-1][...] = p


def dense(x, w, residual):
    n, d = x.shape
    width, bw = w.shape[1], 768
    cols = pl.BlockSpec((n, bw), lambda i: (0, i))
    return pl.pallas_call(
        dense_kernel, out_shape=jax.ShapeDtypeStruct((n, width), BF16), grid=(width // bw,),
        in_specs=[pl.BlockSpec((n, d), lambda i: (0, 0)),
                  pl.BlockSpec((d, bw), lambda i: (0, i))] + [cols] * len(residual),
        out_specs=cols,
        cost_estimate=pl.CostEstimate(flops=2 * n * d * width, bytes_accessed=2 * d * width, transcendentals=0),
    )(x, w, *residual)


def solution(mesh):
    def layer(x_a, route_a, gate_a, h_b, attn_b, route_b, gate_b, w_qkv, w_o, w_gate, w_up, w_down):
        n = x_a.shape[0]
        me = lax.axis_index('ep').astype(I32).reshape(1)
        meta = jnp.concatenate([route_a.T.astype(F32), route_b.T.astype(F32), gate_a.T, gate_b.T], axis=0)
        metas = [meta] + [swap(meta, k) for k in (1, 2, 3)]
        x_par, x_cnt = swap(x_a, 1), swap(x_a, 2)
        mid_b = dense(attn_b, w_o, [h_b])
        b_par, b_cnt = swap(mid_b, 1), swap(mid_b, 2)
        pos, tab, cnt, mid, top = route(me, metas)

        h_loc = up(0, cnt, pos, (x_a, x_par, mid_b, b_par), w_gate, w_up)
        x_cnt, b_cnt = after((x_cnt, b_cnt), h_loc)
        x_dia, b_dia = swap(x_cnt, 1), swap(b_cnt, 1)
        keep, send = ffn(1, cnt, tab, (x_cnt, x_dia, b_cnt, b_dia), w_down, pos=pos, wg=w_gate, wu=w_up)
        got = swap(send, 1)
        there, = mix(there_kernel, mid, (x_cnt, b_cnt), (keep, got), [2 * n])
        back = swap(there, 2)
        keep, send = ffn(0, after(cnt, there), tab, (x_a, x_par, mid_b, b_par), w_down, h_in=h_loc)
        got = swap(send, 1)
        qkv = dense(after(h_b, keep), w_qkv, [])
        out_a, out_b = mix(top_kernel, top, (x_a, mid_b), (keep, got, back), [n, n])
        return out_a, out_b, qkv

    row = P(('dp', 'ep'), None)
    full = P(None, None)
    expert = P('ep', None, None)
    return jax.shard_map(
        layer, mesh=mesh,
        in_specs=(row,) * 7 + (full, full, expert, expert, expert),
        out_specs=(row, row, row), check_vma=False)
```

profile of v0, /device:TPU:0, one launch (start us, length us, event | category | flops | bytes accessed | tf_op | source)
XLA Modules:
  0.0 310.0 jit_solution(6072166165768355121)
XLA Ops:
  0.7 7.9 %shard_map.139.ub0.refs_2_.u1 = bf16[256,2304]{1,0:T(8,128)(2,1)} custom-call(bf16[256,2304]{1,0:T(8,128)(2,1)} %x.1, bf16[2304,2304]{1,0:T(8,128)(2,1)} %w.2, bf16[256,2304]{1,0:T(8,128)(2,1)} %x.2), custom_call_target="tpu_custom_call" | custom-call | flops 2717908992 | bytes 10616832 | tf_op jit(solution)/shard_map/pallas_call | solution.py:362
  8.6 0.8 collective-permute-start.6
  9.4 0.0 copy-start.2
  9.5 2.6 collective-permute-start.2
  12.1 0.4 collective-permute-start.1
  12.5 0.1 collective-permute-start
  12.6 0.9 collective-permute-done.2.m3
  13.4 2.1 collective-permute-start.4
  15.5 0.2 collective-permute-done.1.m2
  15.7 0.4 collective-permute-start.3
  16.1 0.0 collective-permute-done.m1
  16.2 0.2 copy-done.4
  16.3 0.4 copy-done.5
  16.7 3.0 route.1
  19.7 0.0 collective-permute-done.5.ua1.refs_1_
  19.7 48.8 %shard_map.140.refs_4_ = bf16[2,512,5760]{2,1,0:T(8,128)(2,1)} custom-call(s32[2,8,128]{2,1,0:T(8,128)} %get-tuple-element.27.cnt, f32[2,8,256]{2,1,0:T(8,128)} %get-tuple-element.21.pos.refs_0_, bf16[256,2304]{1,0:T(8,128)(2,1)} %u0.1, bf16[256,2304]{1,0:T(8,128)(2,1)} %collective-permute-done.5.ua1.refs_1_, bf16[256,2304]{1,0:T(8,128)(2,1)} %shard_map.139.ub0.refs_2_.u1, ...), custom_call_target="tpu_custom_call" | custom-call | flops 54358179840 | bytes 106168320 | tf_op jit(solution)/shard_map/pallas_call | solution.py:170
  68.5 0.0 collective-permute-done.3.refs_1_.u0
  68.5 18.3 %collective-permute-start.7 = (bf16[256,2304]{1,0:T(8,128)(2,1)}, bf16[256,2304]{1,0:T(8,128)(2,1)}, u32[]{:S(2)}, u32[]{:S(2)}) collective-permute-start(bf16[256,2304]{1,0:T(8,128)(2,1)} %collective-permute-done.3.refs_1_.u0), channel_id=1, source_target_pairs={{0,1},{1,0},{2,3},{3,2},{4,5},{5,4},{6,7},{7,6}} | collective-permute-start | bytes 3538952 | tf_op jit(solution)/shard_map/ppermute | solution.py:23
  86.8 0.0 collective-permute-start.8
  86.9 2.8 collective-permute-done.7.refs_2_
  89.6 1.7 collective-permute-done.8.refs_4_
  91.3 73.9 %shard_map.141 = (bf16[512,2304]{1,0:T(8,128)(2,1)}, bf16[512,2304]{1,0:T(8,128)(2,1)}) custom-call(s32[2,8,128]{2,1,0:T(8,128)} %get-tuple-element.27.cnt, f32[2,256,128]{2,1,0:T(8,128)} %get-tuple-element.24.tab, f32[2,8,256]{2,1,0:T(8,128)} %get-tuple-element.21.pos.refs_0_, bf16[256,2304]{1,0:T(8,128)(2,1)} %collective-permute-done.3.refs_1_.u0, ...), custom_call_target="tpu_custom_call" | custom-call | flops 81537269760 | bytes 159252480 | tf_op jit(solution)/shard_map/pallas_call | solution.py:305
  165.2 29.3 %collective-permute-start.9 = (bf16[512,2304]{1,0:T(8,128)(2,1)}, bf16[512,2304]{1,0:T(8,128)(2,1)S(1)}, u32[]{:S(2)}, u32[]{:S(2)}) collective-permute-start(bf16[512,2304]{1,0:T(8,128)(2,1)} %get-tuple-element.26), channel_id=1, source_target_pairs={{0,1},{1,0},{2,3},{3,2},{4,5},{5,4},{6,7},{7,6}} | collective-permute-start | bytes 7077896 | tf_op jit(solution)/shard_map/ppermute | solution.py:23
  194.5 4.4 %collective-permute-done.9.got = bf16[512,2304]{1,0:T(8,128)(2,1)S(1)} collective-permute-done((bf16[512,2304]{1,0:T(8,128)(2,1)}, bf16[512,2304]{1,0:T(8,128)(2,1)S(1)}, u32[]{:S(2)}, u32[]{:S(2)}) %collective-permute-start.9) | collective-permute-done | bytes 2359328 | tf_op jit(solution)/shard_map/ppermute | solution.py:23
  198.9 1.4 copy-done
  200.2 6.1 %shard_map.142 = bf16[512,2304]{1,0:T(8,128)(2,1)} custom-call(f32[6,256,128]{2,1,0:T(8,128)} %get-tuple-element.20.coef, bf16[256,2304]{1,0:T(8,128)(2,1)} %collective-permute-done.3.refs_1_.u0, bf16[256,2304]{1,0:T(8,128)(2,1)} %collective-permute-done.4.refs_3_.u1, bf16[512,2304]{1,0:T(8,128)(2,1)} %get-tuple-element.25.keep, bf16[512,2304]{1,0:T(8,128)(2,1)} %copy-done), custom_call_target="tpu_custom_call" | custom-call | flops 1000000000 | bytes 1000000 | tf_op jit(solution)/shard_map/pallas_call | solution.py:343
  206.3 35.1 %shard_map.143 = (bf16[512,2304]{1,0:T(8,128)(2,1)}, bf16[512,2304]{1,0:T(8,128)(2,1)}) custom-call(s32[2,8,128]{2,1,0:T(8,128)} %get-tuple-element.27.cnt, f32[2,256,128]{2,1,0:T(8,128)} %get-tuple-element.24.tab, bf16[256,2304]{1,0:T(8,128)(2,1)} %u0.1, bf16[256,2304]{1,0:T(8,128)(2,1)} %collective-permute-done.5.ua1.refs_1_, ...), custom_call_target="tpu_custom_call" | custom-call | flops 27179089920 | bytes 53084160 | tf_op jit(solution)/shard_map/pallas_call | solution.py:305
  241.4 7.6 %collective-permute-start.10 = (bf16[512,2304]{1,0:T(8,128)(2,1)}, bf16[512,2304]{1,0:T(8,128)(2,1)S(1)}, u32[]{:S(2)}, u32[]{:S(2)}) collective-permute-start(bf16[512,2304]{1,0:T(8,128)(2,1)} %get-tuple-element.29), channel_id=1, source_target_pairs={{0,1},{1,0},{2,3},{3,2},{4,5},{5,4},{6,7},{7,6}} | collective-permute-start | bytes 7077896 | tf_op jit(solution)/shard_map/ppermute | solution.py:23
  249.0 0.0 collective-permute-start.11
  249.0 17.6 %shard_map.145 = bf16[256,6912]{1,0:T(8,128)(2,1)} custom-call(bf16[256,2304]{1,0:T(8,128)(2,1)} %x.2, bf16[2304,6912]{1,0:T(8,128)(2,1)} %w.3), custom_call_target="tpu_custom_call" | custom-call | flops 8153726976 | bytes 31850496 | tf_op jit(solution)/shard_map/pallas_call | solution.py:362
  266.6 35.9 %collective-permute-done.11.back = bf16[512,2304]{1,0:T(8,128)(2,1)} collective-permute-done((bf16[512,2304]{1,0:T(8,128)(2,1)}, bf16[512,2304]{1,0:T(8,128)(2,1)}, u32[]{:S(2)}, u32[]{:S(2)}) %collective-permute-start.11) | collective-permute-done | bytes 2359328 | tf_op jit(solution)/shard_map/ppermute | solution.py:23
  302.5 7.5 %shard_map.144 = (bf16[256,2304]{1,0:T(8,128)(2,1)}, bf16[256,2304]{1,0:T(8,128)(2,1)}) custom-call(f32[12,256,128]{2,1,0:T(8,128)} %get-tuple-element.18.coef, bf16[256,2304]{1,0:T(8,128)(2,1)} %u0.1, bf16[256,2304]{1,0:T(8,128)(2,1)} %shard_map.139.ub0.refs_2_.u1, bf16[512,2304]{1,0:T(8,128)(2,1)} %get-tuple-element.28.keep, bf16[512,2304]{1,0:T(8,128)(2,1)} %copy-done.1, ...), custom_call_target="tpu_custom_call" | custom-call | flops 1000000000 | bytes 1000000 | tf_op jit(solution)/shard_map/pallas_call | solution.py:343
  (22 shorter events, 0.1 us)
Async XLA Ops:
  0.6 8.8 %copy-start.6 = (s32[256,2]{0,1:T(2,128)S(1)}, s32[256,2]{0,1:T(2,128)}, u32[]{:S(2)}) copy-start(s32[256,2]{0,1:T(2,128)} %param.17) | copy-start | bytes 6148
  0.6 8.7 %copy-start.7 = (s32[256,2]{0,1:T(2,128)S(1)}, s32[256,2]{0,1:T(2,128)}, u32[]{:S(2)}) copy-start(s32[256,2]{0,1:T(2,128)} %param.13) | copy-start | bytes 6148
  0.7 8.8 %copy-start.8 = (f32[256,2]{0,1:T(2,128)S(1)}, f32[256,2]{0,1:T(2,128)}, u32[]{:S(2)}) copy-start(f32[256,2]{0,1:T(2,128)} %param.18) | copy-start | bytes 6148
  0.7 8.8 %copy-start.9 = (f32[256,2]{0,1:T(2,128)S(1)}, f32[256,2]{0,1:T(2,128)}, u32[]{:S(2)}) copy-start(f32[256,2]{0,1:T(2,128)} %param.14) | copy-start | bytes 6148
  8.6 11.1 %collective-permute-start.6 = (bf16[256,2304]{1,0:T(8,128)(2,1)}, bf16[256,2304]{1,0:T(8,128)(2,1)}, u32[]{:S(2)}, u32[]{:S(2)}) collective-permute-start(bf16[256,2304]{1,0:T(8,128)(2,1)} %shard_map.139.ub0.refs_2_.u1), channel_id=1, source_target_pairs={{0,1},{1,0},{2,3},{3,2},{4,5},{5,4},{6,7},{7,6}} | collective-permute-start | bytes 3538952 | tf_op jit(solution)/shard_map/ppermute | solution.py:23
  9.4 10.3 %collective-permute-start.5 = (bf16[256,2304]{1,0:T(8,128)(2,1)}, bf16[256,2304]{1,0:T(8,128)(2,1)}, u32[]{:S(2)}, u32[]{:S(2)}) collective-permute-start(bf16[256,2304]{1,0:T(8,128)(2,1)} %u0.1), channel_id=1, source_target_pairs={{0,1},{1,0},{2,3},{3,2},{4,5},{5,4},{6,7},{7,6}} | collective-permute-start | bytes 3538952 | tf_op jit(solution)/shard_map/ppermute | solution.py:23
  9.4 6.7 %copy-start.2 = (f32[8,256]{1,0:T(8,128)}, f32[8,256]{1,0:T(8,128)S(1)}, u32[]{:S(2)}) copy-start(f32[8,256]{1,0:T(8,128)S(1)} %pad_maximum_fusion.m0) | copy-start | bytes 24580
  9.5 4.0 %collective-permute-start.2 = (f32[8,256]{1,0:T(8,128)S(1)}, f32[8,256]{1,0:T(8,128)S(1)}, u32[]{:S(2)}, u32[]{:S(2)}) collective-permute-start(f32[8,256]{1,0:T(8,128)S(1)} %pad_maximum_fusion.m0), channel_id=1, source_target_pairs={{0,3},{1,2},{2,1},{3,0},{4,7},{5,6},{6,5},{7,4}} | collective-permute-start | bytes 24584 | tf_op jit(solution)/shard_map/ppermute | solution.py:23
  12.1 3.7 %collective-permute-start.1 = (f32[8,256]{1,0:T(8,128)S(1)}, f32[8,256]{1,0:T(8,128)S(1)}, u32[]{:S(2)}, u32[]{:S(2)}) collective-permute-start(f32[8,256]{1,0:T(8,128)S(1)} %pad_maximum_fusion.m0), channel_id=1, source_target_pairs={{0,2},{1,3},{2,0},{3,1},{4,6},{5,7},{6,4},{7,5}} | collective-permute-start | bytes 24584 | tf_op jit(solution)/shard_map/ppermute | solution.py:23
  12.5 3.7 %collective-permute-start = (f32[8,256]{1,0:T(8,128)S(1)}, f32[8,256]{1,0:T(8,128)S(1)}, u32[]{:S(2)}, u32[]{:S(2)}) collective-permute-start(f32[8,256]{1,0:T(8,128)S(1)} %pad_maximum_fusion.m0), channel_id=1, source_target_pairs={{0,1},{1,0},{2,3},{3,2},{4,5},{5,4},{6,7},{7,6}} | collective-permute-start | bytes 24584 | tf_op jit(solution)/shard_map/ppermute | solution.py:23
  13.4 2.7 copy-start.3
  13.4 55.1 %collective-permute-start.4 = (bf16[256,2304]{1,0:T(8,128)(2,1)}, bf16[256,2304]{1,0:T(8,128)(2,1)}, u32[]{:S(2)}, u32[]{:S(2)}) collective-permute-start(bf16[256,2304]{1,0:T(8,128)(2,1)} %shard_map.139.ub0.refs_2_.u1), channel_id=1, source_target_pairs={{0,2},{1,3},{2,0},{3,1},{4,6},{5,7},{6,4},{7,5}} | collective-permute-start | bytes 3538952 | tf_op jit(solution)/shard_map/ppermute | solution.py:23
  15.7 0.6 copy-start.4
  15.7 52.8 %collective-permute-start.3 = (bf16[256,2304]{1,0:T(8,128)(2,1)}, bf16[256,2304]{1,0:T(8,128)(2,1)}, u32[]{:S(2)}, u32[]{:S(2)}) collective-permute-start(bf16[256,2304]{1,0:T(8,128)(2,1)} %u0.1), channel_id=1, source_target_pairs={{0,2},{1,3},{2,0},{3,1},{4,6},{5,7},{6,4},{7,5}} | collective-permute-start | bytes 3538952 | tf_op jit(solution)/shard_map/ppermute | solution.py:23
  16.1 0.6 copy-start.5
  68.5 21.1 %collective-permute-start.7 = (bf16[256,2304]{1,0:T(8,128)(2,1)}, bf16[256,2304]{1,0:T(8,128)(2,1)}, u32[]{:S(2)}, u32[]{:S(2)}) collective-permute-start(bf16[256,2304]{1,0:T(8,128)(2,1)} %collective-permute-done.3.refs_1_.u0), channel_id=1, source_target_pairs={{0,1},{1,0},{2,3},{3,2},{4,5},{5,4},{6,7},{7,6}} | collective-permute-start | bytes 3538952 | tf_op jit(solution)/shard_map/ppermute | solution.py:23
  86.8 4.5 %collective-permute-start.8 = (bf16[256,2304]{1,0:T(8,128)(2,1)}, bf16[256,2304]{1,0:T(8,128)(2,1)}, u32[]{:S(2)}, u32[]{:S(2)}) collective-permute-start(bf16[256,2304]{1,0:T(8,128)(2,1)} %collective-permute-done.4.refs_3_.u1), channel_id=1, source_target_pairs={{0,1},{1,0},{2,3},{3,2},{4,5},{5,4},{6,7},{7,6}} | collective-permute-start | bytes 3538952 | tf_op jit(solution)/shard_map/ppermute | solution.py:23
  165.2 33.7 %collective-permute-start.9 = (bf16[512,2304]{1,0:T(8,128)(2,1)}, bf16[512,2304]{1,0:T(8,128)(2,1)S(1)}, u32[]{:S(2)}, u32[]{:S(2)}) collective-permute-start(bf16[512,2304]{1,0:T(8,128)(2,1)} %get-tuple-element.26), channel_id=1, source_target_pairs={{0,1},{1,0},{2,3},{3,2},{4,5},{5,4},{6,7},{7,6}} | collective-permute-start | bytes 7077896 | tf_op jit(solution)/shard_map/ppermute | solution.py:23
  198.9 1.4 copy-start
  241.4 25.2 %collective-permute-start.10 = (bf16[512,2304]{1,0:T(8,128)(2,1)}, bf16[512,2304]{1,0:T(8,128)(2,1)S(1)}, u32[]{:S(2)}, u32[]{:S(2)}) collective-permute-start(bf16[512,2304]{1,0:T(8,128)(2,1)} %get-tuple-element.29), channel_id=1, source_target_pairs={{0,1},{1,0},{2,3},{3,2},{4,5},{5,4},{6,7},{7,6}} | collective-permute-start | bytes 7077896 | tf_op jit(solution)/shard_map/ppermute | solution.py:23
  249.0 53.5 %collective-permute-start.11 = (bf16[512,2304]{1,0:T(8,128)(2,1)}, bf16[512,2304]{1,0:T(8,128)(2,1)}, u32[]{:S(2)}, u32[]{:S(2)}) collective-permute-start(bf16[512,2304]{1,0:T(8,128)(2,1)} %shard_map.142), channel_id=1, source_target_pairs={{0,2},{1,3},{2,0},{3,1},{4,6},{5,7},{6,4},{7,5}} | collective-permute-start | bytes 7077896 | tf_op jit(solution)/shard_map/ppermute | solution.py:23
  266.6 35.9 %copy-start.1 = (bf16[512,2304]{1,0:T(8,128)(2,1)}, bf16[512,2304]{1,0:T(8,128)(2,1)S(1)}, u32[]{:S(2)}) copy-start(bf16[512,2304]{1,0:T(8,128)(2,1)S(1)} %collective-permute-done.10.got) | copy-start | bytes 7077892
where the time goes:
time: 311 us; the launch traced here: 310 us
  Pallas kernels  200 us (64%)
  starting transfers between devices  61.7 us (20%)
  waiting for transfers between devices  45.9 us (15%)
    pallas_call x2, Pallas kernels, ffn(): pl.pallas_call(functools.partial(ffn_kernel, loc, n1, nc), out_shape=[out...  109 us
    ppermute x12, starting transfers between devices, swap(): return lax.ppermute(x, 'ep', [(i, i ^ k) for i in range(N_SRC)])  61.7 us
    pallas_call x1, Pallas kernels, up(): pl.pallas_call(functools.partial(up_kernel, loc, ff // FC), out_shape=jax...  48.8 us
    ppermute x12, waiting for transfers between devices, swap(): return lax.ppermute(x, 'ep', [(i, i ^ k) for i in range(N_SRC)])  45.9 us
    pallas_call x2, Pallas kernels, dense(): pl.pallas_call(dense_kernel, out_shape=jax.ShapeDtypeStruct((n, width), B...  25.4 us
    pallas_call x2, Pallas kernels, mix(): pl.pallas_call(kernel, out_shape=[jax.ShapeDtypeStruct((r, d), BF16) for...  13.6 us
  transfers between devices with their start and end apart: 12, of which 6 were waited for; matrix products, arithmetic and copies ran while one was open for 0% of the time, Pallas kernels for 22%

commit v1 on v0

--- a/solution.py
+++ b/solution.py
@@ -27,7 +27,7 @@
     return lax.optimization_barrier((x, dep))[0]
 
 
-def route_kernel(me_ref, m0, m1, m2, m3, pos_ref, tab_ref, cnt_ref, mid_ref, top_ref):
+def route_kernel(me_ref, m0, m1, m2, m3, pos_ref, tab_ref, cnt_ref):
     me = me_ref[0]
     n_tok = m0.shape[1]
     before = (lax.broadcasted_iota(I32, (n_tok, n_tok), 0)
@@ -76,12 +76,25 @@
         rows += coefs(jnp.logical_and(c2[0] == 1.0, c2[1] == 1.0), g2[:2])
         rows += coefs(c[0] + c[1] == 1.0, [g[0] + g[1], g[2] + g[3]])
         rows = jnp.concatenate(rows + [jnp.zeros((128 - COL_TOP - 3, n_tok), F32)], axis=0)
-        t = rows.T
-        tab_ref[mb] = t
+        tab_ref[mb] = rows.T
+
+
+def spread_kernel(tab, mid_ref, top_ref):
+    for mb in range(2):
+        t = tab[mb]
         for ref, cols in ((mid_ref, range(COL_CNT, COL_CNT + 3)),
                           (top_ref, [*range(COL_OWN, COL_OWN + 3), *range(COL_TOP, COL_TOP + 3)])):
             for k, c in enumerate(cols):
-                ref[len(cols) * mb + k] = jnp.broadcast_to(t[:, c:c + 1], (n_tok, 128))
+                ref[len(cols) * mb + k] = jnp.broadcast_to(t[:, c:c + 1], (t.shape[0], 128))
+
+
+def spread(tab):
+    n_tok = tab.shape[1]
+    return pl.pallas_call(
+        spread_kernel,
+        out_shape=[jax.ShapeDtypeStruct((k, n_tok, 128), F32) for k in (6, 12)],
+        cost_estimate=pl.CostEstimate(flops=10 ** 8, bytes_accessed=10 ** 6, transcendentals=0), name='spread',
+    )(tab)
 
 
 def route(me, metas):
@@ -89,10 +102,9 @@
     return pl.pallas_call(
         route_kernel,
         out_shape=[jax.ShapeDtypeStruct((2, 8, n_tok), F32), jax.ShapeDtypeStruct((2, n_tok, 128), F32),
-                   jax.ShapeDtypeStruct((2, 8, 128), I32), jax.ShapeDtypeStruct((6, n_tok, 128), F32),
-                   jax.ShapeDtypeStruct((12, n_tok, 128), F32)],
+                   jax.ShapeDtypeStruct((2, 8, 128), I32)],
         in_specs=[pl.BlockSpec(memory_space=pltpu.SMEM)] + [pl.BlockSpec(memory_space=pltpu.VMEM)] * 4,
-        out_specs=[pl.BlockSpec(memory_space=pltpu.VMEM)] * 5,
+        out_specs=[pl.BlockSpec(memory_space=pltpu.VMEM)] * 3,
         name='route',
     )(me, *metas)
 
@@ -121,19 +133,25 @@
         return [pltpu.make_async_copy(wg.at[l, :, cols], w.at[s, :, pl.ds(0, FC)], sem.at[s, 0]),
                 pltpu.make_async_copy(wu.at[l, :, cols], w.at[s, :, pl.ds(FC, FC)], sem.at[s, 1])]
 
+    def gather(l):
+        x[l] = jnp.zeros(x.shape[1:], BF16)
+        for k in range(4):
+            q = l * N_SRC + 2 * loc + k % 2
+            p = pos[k // 2, q:q + 1, :]
+            pick = (lax.broadcasted_iota(I32, (SLOTS, p.shape[1]), 0).astype(F32) == p).astype(BF16)
+            rows = jnp.dot(pick, us[k][...], preferred_element_type=F32)
+            x[l, pl.ds(pl.multiple_of(offset(cnt, l, loc, k), 16), SLOTS), :] = rows.astype(BF16)
+
     @pl.when(i == 0)
     def _():
         for j in range(ns - 1):
             for c in copies(j):
                 c.start()
-        x[...] = jnp.zeros_like(x)
-        for l in range(2):
-            for k in range(4):
-                q = l * N_SRC + 2 * loc + k % 2
-                p = pos[k // 2, q:q + 1, :]
-                pick = (lax.broadcasted_iota(I32, (SLOTS, p.shape[1]), 0).astype(F32) == p).astype(BF16)
-                rows = jnp.dot(pick, us[k][...], preferred_element_type=F32)
-                x[l, pl.ds(pl.multiple_of(offset(cnt, l, loc, k), 16), SLOTS), :] = rows.astype(BF16)
+        gather(0)
+
+    @pl.when(i == 1)
+    def _():
+        gather(1)
 
     @pl.when(i + ns - 1 < n)
     def _():
@@ -338,12 +356,13 @@
 
 def mix(kernel, coef, us, rows, outs):
     n, d = us[0].shape
-    bw = 768
+    bw = 384
     at = lambda r: pl.BlockSpec((r, bw), lambda i: (0, i))
     return pl.pallas_call(
         kernel, out_shape=[jax.ShapeDtypeStruct((r, d), BF16) for r in outs], grid=(d // bw,),
         in_specs=[pl.BlockSpec(coef.shape, lambda i: (0, 0, 0))] + [at(n)] * 2 + [at(2 * n)] * len(rows),
         out_specs=[at(r) for r in outs],
+        compiler_params=pltpu.CompilerParams(vmem_limit_bytes=67043328),
         cost_estimate=pl.CostEstimate(flops=10 ** 9, bytes_accessed=10 ** 6, transcendentals=0),
     )(coef, *us, *rows)
 
@@ -377,12 +396,13 @@
         x_par, x_cnt = swap(x_a, 1), swap(x_a, 2)
         mid_b = dense(attn_b, w_o, [h_b])
         b_par, b_cnt = swap(mid_b, 1), swap(mid_b, 2)
-        pos, tab, cnt, mid, top = route(me, metas)
+        pos, tab, cnt = route(me, metas)
 
         h_loc = up(0, cnt, pos, (x_a, x_par, mid_b, b_par), w_gate, w_up)
         x_cnt, b_cnt = after((x_cnt, b_cnt), h_loc)
         x_dia, b_dia = swap(x_cnt, 1), swap(b_cnt, 1)
-        keep, send = ffn(1, cnt, tab, (x_cnt, x_dia, b_cnt, b_dia), w_down, pos=pos, wg=w_gate, wu=w_up)
+        mid, top = spread(after(tab, h_loc))
+        keep, send = ffn(1, after(cnt, mid), tab, (x_cnt, x_dia, b_cnt, b_dia), w_down, pos=pos, wg=w_gate, wu=w_up)
         got = swap(send, 1)
         there, = mix(there_kernel, mid, (x_cnt, b_cnt), (keep, got), [2 * n])
         back = swap(there, 2)

time: 311 us -> 310 us (level)
  transfers between devices with their start and end apart: 12 -> 12, of which waited for: 6 -> 6; matrix products, arithmetic and copies ran while one was open for 0% -> 0% of each run, Pallas kernels for 22% -> 23%
where the time goes in v1:
time: 310 us; the launch traced here: 309 us
  Pallas kernels  202 us (65%)
  starting transfers between devices  61.9 us (20%)
  waiting for transfers between devices  43.9 us (14%)
    pallas_call x2, Pallas kernels, ffn(): pl.pallas_call(functools.partial(ffn_kernel, loc, n1, nc), out_shape=[out...  109 us
    ppermute x12, starting transfers between devices, swap(): return lax.ppermute(x, 'ep', [(i, i ^ k) for i in range(N_SRC)])  61.9 us
    pallas_call x1, Pallas kernels, up(): pl.pallas_call(functools.partial(up_kernel, loc, ff // FC), out_shape=jax...  48.1 us
    ppermute x12, waiting for transfers between devices, swap(): return lax.ppermute(x, 'ep', [(i, i ^ k) for i in range(N_SRC)])  43.9 us
    pallas_call x2, Pallas kernels, dense(): pl.pallas_call(dense_kernel, out_shape=jax.ShapeDtypeStruct((n, width), B...  25.4 us
    pallas_call x2, Pallas kernels, mix(): pl.pallas_call(kernel, out_shape=[jax.ShapeDtypeStruct((r, d), BF16) for...  14.7 us
  transfers between devices with their start and end apart: 12, of which 6 were waited for; matrix products, arithmetic and copies ran while one was open for 0% of the time, Pallas kernels for 23%

profile of v1, /device:TPU:0, one launch (start us, length us, event | category | flops | bytes accessed | tf_op | source)
XLA Modules:
  0.0 309.1 jit_solution(11011955793471027988)
XLA Ops:
  0.7 7.8 %shard_map.139.ub0.refs_2_.u1 = bf16[256,2304]{1,0:T(8,128)(2,1)} custom-call(bf16[256,2304]{1,0:T(8,128)(2,1)} %x.1, bf16[2304,2304]{1,0:T(8,128)(2,1)} %w.2, bf16[256,2304]{1,0:T(8,128)(2,1)} %x.2), custom_call_target="tpu_custom_call" | custom-call | flops 2717908992 | bytes 10616832 | tf_op jit(solution)/shard_map/pallas_call | solution.py:381
  8.5 0.8 collective-permute-start.4
  9.3 0.0 collective-permute-start.3
  9.4 0.0 copy-start
  9.4 2.6 collective-permute-start.2
  12.0 0.4 collective-permute-start.1
  12.4 0.1 collective-permute-start
  12.5 0.9 collective-permute-done.2.m3
  13.4 2.1 collective-permute-start.6
  15.5 0.2 collective-permute-done.1.m2
  15.7 0.4 collective-permute-start.5
  16.1 0.0 collective-permute-done.m1
  16.1 0.2 copy-done.2
  16.3 0.4 copy-done.3
  16.7 1.7 route.1
  18.4 0.0 collective-permute-done.4.ub1.refs_3_
  18.4 0.0 collective-permute-done.3.ua1.refs_1_
  18.4 48.1 %shard_map.140.refs_4_ = bf16[2,512,5760]{2,1,0:T(8,128)(2,1)} custom-call(s32[2,8,128]{2,1,0:T(8,128)} %get-tuple-element.31.cnt, f32[2,8,256]{2,1,0:T(8,128)} %get-tuple-element.22.pos.refs_0_, bf16[256,2304]{1,0:T(8,128)(2,1)} %u0.1, bf16[256,2304]{1,0:T(8,128)(2,1)} %collective-permute-done.3.ua1.refs_1_, bf16[256,2304]{1,0:T(8,128)(2,1)} %shard_map.139.ub0.refs_2_.u1, ...), custom_call_target="tpu_custom_call" | custom-call | flops 54358179840 | bytes 106168320 | tf_op jit(solution)/shard_map/pallas_call | solution.py:188
  66.5 0.8 collective-permute-done.5.refs_1_.u0
  67.3 18.4 %collective-permute-start.7 = (bf16[256,2304]{1,0:T(8,128)(2,1)}, bf16[256,2304]{1,0:T(8,128)(2,1)}, u32[]{:S(2)}, u32[]{:S(2)}) collective-permute-start(bf16[256,2304]{1,0:T(8,128)(2,1)} %collective-permute-done.5.refs_1_.u0), channel_id=1, source_target_pairs={{0,1},{1,0},{2,3},{3,2},{4,5},{5,4},{6,7},{7,6}} | collective-permute-start | bytes 3538952 | tf_op jit(solution)/shard_map/ppermute | solution.py:23
  85.8 0.0 collective-permute-start.8
  85.8 2.8 spread.1
  88.6 1.6 collective-permute-done.8.refs_4_
  90.3 74.0 %shard_map.141 = (bf16[512,2304]{1,0:T(8,128)(2,1)}, bf16[512,2304]{1,0:T(8,128)(2,1)}) custom-call(s32[2,8,128]{2,1,0:T(8,128)} %get-tuple-element.31.cnt, f32[2,256,128]{2,1,0:T(8,128)} %get-tuple-element.23.tab, f32[2,8,256]{2,1,0:T(8,128)} %get-tuple-element.22.pos.refs_0_, bf16[256,2304]{1,0:T(8,128)(2,1)} %collective-permute-done.5.refs_1_.u0, ...), custom_call_target="tpu_custom_call" | custom-call | flops 81537269760 | bytes 159252480 | tf_op jit(solution)/shard_map/pallas_call | solution.py:323
  164.3 29.4 %collective-permute-start.9 = (bf16[512,2304]{1,0:T(8,128)(2,1)}, bf16[512,2304]{1,0:T(8,128)(2,1)}, u32[]{:S(2)}, u32[]{:S(2)}) collective-permute-start(bf16[512,2304]{1,0:T(8,128)(2,1)} %get-tuple-element.30), channel_id=1, source_target_pairs={{0,1},{1,0},{2,3},{3,2},{4,5},{5,4},{6,7},{7,6}} | collective-permute-start | bytes 7077896 | tf_op jit(solution)/shard_map/ppermute | solution.py:23
  193.7 4.5 %collective-permute-done.9.got = bf16[512,2304]{1,0:T(8,128)(2,1)} collective-permute-done((bf16[512,2304]{1,0:T(8,128)(2,1)}, bf16[512,2304]{1,0:T(8,128)(2,1)}, u32[]{:S(2)}, u32[]{:S(2)}) %collective-permute-start.9) | collective-permute-done | bytes 2359328 | tf_op jit(solution)/shard_map/ppermute | solution.py:23
  198.2 6.8 %shard_map.142 = bf16[512,2304]{1,0:T(8,128)(2,1)} custom-call(f32[6,256,128]{2,1,0:T(8,128)} %get-tuple-element.25.coef, bf16[256,2304]{1,0:T(8,128)(2,1)} %collective-permute-done.5.refs_1_.u0, bf16[256,2304]{1,0:T(8,128)(2,1)} %collective-permute-done.6.refs_3_.u1, bf16[512,2304]{1,0:T(8,128)(2,1)} %get-tuple-element.29.keep, ...), custom_call_target="tpu_custom_call" | custom-call | flops 1000000000 | bytes 1000000 | tf_op jit(solution)/shard_map/pallas_call | solution.py:361
  205.0 35.1 %shard_map.143 = (bf16[512,2304]{1,0:T(8,128)(2,1)}, bf16[512,2304]{1,0:T(8,128)(2,1)}) custom-call(s32[2,8,128]{2,1,0:T(8,128)} %get-tuple-element.31.cnt, f32[2,256,128]{2,1,0:T(8,128)} %get-tuple-element.23.tab, bf16[256,2304]{1,0:T(8,128)(2,1)} %u0.1, bf16[256,2304]{1,0:T(8,128)(2,1)} %collective-permute-done.3.ua1.refs_1_, ...), custom_call_target="tpu_custom_call" | custom-call | flops 27179089920 | bytes 53084160 | tf_op jit(solution)/shard_map/pallas_call | solution.py:323
  240.1 7.6 %collective-permute-start.10 = (bf16[512,2304]{1,0:T(8,128)(2,1)}, bf16[512,2304]{1,0:T(8,128)(2,1)}, u32[]{:S(2)}, u32[]{:S(2)}) collective-permute-start(bf16[512,2304]{1,0:T(8,128)(2,1)} %get-tuple-element.33), channel_id=1, source_target_pairs={{0,1},{1,0},{2,3},{3,2},{4,5},{5,4},{6,7},{7,6}} | collective-permute-start | bytes 7077896 | tf_op jit(solution)/shard_map/ppermute | solution.py:23
  247.7 17.6 %shard_map.145 = bf16[256,6912]{1,0:T(8,128)(2,1)} custom-call(bf16[256,2304]{1,0:T(8,128)(2,1)} %x.2, bf16[2304,6912]{1,0:T(8,128)(2,1)} %w.3), custom_call_target="tpu_custom_call" | custom-call | flops 8153726976 | bytes 31850496 | tf_op jit(solution)/shard_map/pallas_call | solution.py:381
  265.3 35.9 %collective-permute-done.11.back = bf16[512,2304]{1,0:T(8,128)(2,1)} collective-permute-done((bf16[512,2304]{1,0:T(8,128)(2,1)}, bf16[512,2304]{1,0:T(8,128)(2,1)}, u32[]{:S(2)}, u32[]{:S(2)}) %collective-permute-start.11) | collective-permute-done | bytes 2359328 | tf_op jit(solution)/shard_map/ppermute | solution.py:23
  301.2 7.9 %shard_map.144 = (bf16[256,2304]{1,0:T(8,128)(2,1)}, bf16[256,2304]{1,0:T(8,128)(2,1)}) custom-call(f32[12,256,128]{2,1,0:T(8,128)} %get-tuple-element.24.coef, bf16[256,2304]{1,0:T(8,128)(2,1)} %u0.1, bf16[256,2304]{1,0:T(8,128)(2,1)} %shard_map.139.ub0.refs_2_.u1, bf16[512,2304]{1,0:T(8,128)(2,1)} %get-tuple-element.32.keep, ...), custom_call_target="tpu_custom_call" | custom-call | flops 1000000000 | bytes 1000000 | tf_op jit(solution)/shard_map/pallas_call | solution.py:361
  (19 shorter events, 0.1 us)
Async XLA Ops:
  0.6 8.7 %copy-start.4 = (s32[256,2]{0,1:T(2,128)S(1)}, s32[256,2]{0,1:T(2,128)}, u32[]{:S(2)}) copy-start(s32[256,2]{0,1:T(2,128)} %param.17) | copy-start | bytes 6148
  0.6 8.7 %copy-start.5 = (s32[256,2]{0,1:T(2,128)S(1)}, s32[256,2]{0,1:T(2,128)}, u32[]{:S(2)}) copy-start(s32[256,2]{0,1:T(2,128)} %param.13) | copy-start | bytes 6148
  0.7 8.7 %copy-start.6 = (f32[256,2]{0,1:T(2,128)S(1)}, f32[256,2]{0,1:T(2,128)}, u32[]{:S(2)}) copy-start(f32[256,2]{0,1:T(2,128)} %param.18) | copy-start | bytes 6148
  0.7 8.7 %copy-start.7 = (f32[256,2]{0,1:T(2,128)S(1)}, f32[256,2]{0,1:T(2,128)}, u32[]{:S(2)}) copy-start(f32[256,2]{0,1:T(2,128)} %param.14) | copy-start | bytes 6148
  8.5 9.9 %collective-permute-start.4 = (bf16[256,2304]{1,0:T(8,128)(2,1)}, bf16[256,2304]{1,0:T(8,128)(2,1)}, u32[]{:S(2)}, u32[]{:S(2)}) collective-permute-start(bf16[256,2304]{1,0:T(8,128)(2,1)} %shard_map.139.ub0.refs_2_.u1), channel_id=1, source_target_pairs={{0,1},{1,0},{2,3},{3,2},{4,5},{5,4},{6,7},{7,6}} | collective-permute-start | bytes 3538952 | tf_op jit(solution)/shard_map/ppermute | solution.py:23
  9.3 9.1 %collective-permute-start.3 = (bf16[256,2304]{1,0:T(8,128)(2,1)}, bf16[256,2304]{1,0:T(8,128)(2,1)}, u32[]{:S(2)}, u32[]{:S(2)}) collective-permute-start(bf16[256,2304]{1,0:T(8,128)(2,1)} %u0.1), channel_id=1, source_target_pairs={{0,1},{1,0},{2,3},{3,2},{4,5},{5,4},{6,7},{7,6}} | collective-permute-start | bytes 3538952 | tf_op jit(solution)/shard_map/ppermute | solution.py:23
  9.4 6.7 %copy-start = (f32[8,256]{1,0:T(8,128)}, f32[8,256]{1,0:T(8,128)S(1)}, u32[]{:S(2)}) copy-start(f32[8,256]{1,0:T(8,128)S(1)} %pad_maximum_fusion.m0) | copy-start | bytes 24580
  9.4 4.0 %collective-permute-start.2 = (f32[8,256]{1,0:T(8,128)S(1)}, f32[8,256]{1,0:T(8,128)S(1)}, u32[]{:S(2)}, u32[]{:S(2)}) collective-permute-start(f32[8,256]{1,0:T(8,128)S(1)} %pad_maximum_fusion.m0), channel_id=1, source_target_pairs={{0,3},{1,2},{2,1},{3,0},{4,7},{5,6},{6,5},{7,4}} | collective-permute-start | bytes 24584 | tf_op jit(solution)/shard_map/ppermute | solution.py:23
  12.0 3.7 %collective-permute-start.1 = (f32[8,256]{1,0:T(8,128)S(1)}, f32[8,256]{1,0:T(8,128)S(1)}, u32[]{:S(2)}, u32[]{:S(2)}) collective-permute-start(f32[8,256]{1,0:T(8,128)S(1)} %pad_maximum_fusion.m0), channel_id=1, source_target_pairs={{0,2},{1,3},{2,0},{3,1},{4,6},{5,7},{6,4},{7,5}} | collective-permute-start | bytes 24584 | tf_op jit(solution)/shard_map/ppermute | solution.py:23
  12.4 3.7 %collective-permute-start = (f32[8,256]{1,0:T(8,128)S(1)}, f32[8,256]{1,0:T(8,128)S(1)}, u32[]{:S(2)}, u32[]{:S(2)}) collective-permute-start(f32[8,256]{1,0:T(8,128)S(1)} %pad_maximum_fusion.m0), channel_id=1, source_target_pairs={{0,1},{1,0},{2,3},{3,2},{4,5},{5,4},{6,7},{7,6}} | collective-permute-start | bytes 24584 | tf_op jit(solution)/shard_map/ppermute | solution.py:23
  13.4 2.7 copy-start.1
  13.4 53.1 %collective-permute-start.6 = (bf16[256,2304]{1,0:T(8,128)(2,1)}, bf16[256,2304]{1,0:T(8,128)(2,1)}, u32[]{:S(2)}, u32[]{:S(2)}) collective-permute-start(bf16[256,2304]{1,0:T(8,128)(2,1)} %shard_map.139.ub0.refs_2_.u1), channel_id=1, source_target_pairs={{0,2},{1,3},{2,0},{3,1},{4,6},{5,7},{6,4},{7,5}} | collective-permute-start | bytes 3538952 | tf_op jit(solution)/shard_map/ppermute | solution.py:23
  15.7 0.6 copy-start.2
  15.7 51.7 %collective-permute-start.5 = (bf16[256,2304]{1,0:T(8,128)(2,1)}, bf16[256,2304]{1,0:T(8,128)(2,1)}, u32[]{:S(2)}, u32[]{:S(2)}) collective-permute-start(bf16[256,2304]{1,0:T(8,128)(2,1)} %u0.1), channel_id=1, source_target_pairs={{0,2},{1,3},{2,0},{3,1},{4,6},{5,7},{6,4},{7,5}} | collective-permute-start | bytes 3538952 | tf_op jit(solution)/shard_map/ppermute | solution.py:23
  16.1 0.6 copy-start.3
  67.3 21.3 %collective-permute-start.7 = (bf16[256,2304]{1,0:T(8,128)(2,1)}, bf16[256,2304]{1,0:T(8,128)(2,1)}, u32[]{:S(2)}, u32[]{:S(2)}) collective-permute-start(bf16[256,2304]{1,0:T(8,128)(2,1)} %collective-permute-done.5.refs_1_.u0), channel_id=1, source_target_pairs={{0,1},{1,0},{2,3},{3,2},{4,5},{5,4},{6,7},{7,6}} | collective-permute-start | bytes 3538952 | tf_op jit(solution)/shard_map/ppermute | solution.py:23
  85.8 4.5 %collective-permute-start.8 = (bf16[256,2304]{1,0:T(8,128)(2,1)}, bf16[256,2304]{1,0:T(8,128)(2,1)}, u32[]{:S(2)}, u32[]{:S(2)}) collective-permute-start(bf16[256,2304]{1,0:T(8,128)(2,1)} %collective-permute-done.6.refs_3_.u1), channel_id=1, source_target_pairs={{0,1},{1,0},{2,3},{3,2},{4,5},{5,4},{6,7},{7,6}} | collective-permute-start | bytes 3538952 | tf_op jit(solution)/shard_map/ppermute | solution.py:23
  164.3 33.9 %collective-permute-start.9 = (bf16[512,2304]{1,0:T(8,128)(2,1)}, bf16[512,2304]{1,0:T(8,128)(2,1)}, u32[]{:S(2)}, u32[]{:S(2)}) collective-permute-start(bf16[512,2304]{1,0:T(8,128)(2,1)} %get-tuple-element.30), channel_id=1, source_target_pairs={{0,1},{1,0},{2,3},{3,2},{4,5},{5,4},{6,7},{7,6}} | collective-permute-start | bytes 7077896 | tf_op jit(solution)/shard_map/ppermute | solution.py:23
  240.1 25.2 %collective-permute-start.10 = (bf16[512,2304]{1,0:T(8,128)(2,1)}, bf16[512,2304]{1,0:T(8,128)(2,1)}, u32[]{:S(2)}, u32[]{:S(2)}) collective-permute-start(bf16[512,2304]{1,0:T(8,128)(2,1)} %get-tuple-element.33), channel_id=1, source_target_pairs={{0,1},{1,0},{2,3},{3,2},{4,5},{5,4},{6,7},{7,6}} | collective-permute-start | bytes 7077896 | tf_op jit(solution)/shard_map/ppermute | solution.py:23
  247.7 53.5 %collective-permute-start.11 = (bf16[512,2304]{1,0:T(8,128)(2,1)}, bf16[512,2304]{1,0:T(8,128)(2,1)}, u32[]{:S(2)}, u32[]{:S(2)}) collective-permute-start(bf16[512,2304]{1,0:T(8,128)(2,1)} %shard_map.142), channel_id=1, source_target_pairs={{0,2},{1,3},{2,0},{3,1},{4,6},{5,7},{6,4},{7,5}} | collective-permute-start | bytes 7077896 | tf_op jit(solution)/shard_map/ppermute | solution.py:23

commit v2 on v1

--- a/solution.py
+++ b/solution.py
@@ -198,19 +198,21 @@
     )(cnt, pos, *us, wg, wu)
 
 
-def ffn_kernel(loc, n1, nc, cnt, tab, *refs):
+def ffn_kernel(loc, n0, n1, nc, cnt, tab, *refs):
     it = iter(refs)
     pos = next(it) if n1 else None
     us = [next(it) for _ in range(4)]
     wg, wu = (next(it), next(it)) if n1 else (None, None)
-    h_in = None if n1 else next(it)
-    wd, keep, send, h, y, w2, pick, coef, s2 = [next(it) for _ in range(9)]
+    h_in, xd, wq = (None, None, None) if n1 else [next(it) for _ in range(3)]
+    wd, keep, send = next(it), next(it), next(it)
+    dense_out = None if n1 else next(it)
+    h, y, w2, pick, coef, s2 = [next(it) for _ in range(6)]
     x, w1, s1 = [next(it) for _ in range(3)] if n1 else (None,) * 3
-    sh = None if n1 else next(it)
+    w0, s0, sh = (None, None, None) if n1 else [next(it) for _ in range(3)]
     i = pl.program_id(0)
     n_tok = tab.shape[1]
-    j = i - n1
-    n2 = pl.num_programs(0) - n1
+    j = i - n1 - n0
+    n2 = pl.num_programs(0) - n1 - n0
 
     def copy2(j):
         cols = pl.ds(pl.multiple_of(lax.div(j, 2) * DC, 128), DC)
@@ -223,10 +225,35 @@
         for_rows(offset(cnt, e, loc, 4), lambda rows: act(h_copy(e, rows)))
 
     if not n1:
+        def copy0(j):
+            cols = pl.ds(pl.multiple_of(j * DC, 128), DC)
+            return pltpu.make_async_copy(wq.at[:, cols], w0.at[lax.rem(j, 3)], s0.at[lax.rem(j, 3)])
+
         @pl.when(i == 0)
         def _():
+            copy0(0).start()
+            copy0(1).start()
+
+        @pl.when(i + 2 < n0)
+        def _():
+            copy0(i + 2).start()
+
+        @pl.when(i == 2)
+        def _():
             h_copies(0, lambda c: c.start())
+
+        @pl.when(i == 4)
+        def _():
+            h_copies(1, lambda c: c.start())
+
+        @pl.when(i == 6)
+        def _():
             copy2(0).start()
+
+        @pl.when(i < n0)
+        def _():
+            copy0(i).wait()
+            dense_out[...] = jnp.dot(xd[...], w0[lax.rem(i, 3)], preferred_element_type=F32).astype(BF16)
 
     @pl.when(i == 0)
     def _():
@@ -254,14 +281,9 @@
     def _():
         l = lax.rem(j, 2)
         if not n1:
-            @pl.when(j == 0)
+            @pl.when(j < 2)
             def _():
-                h_copies(0, lambda c: c.wait())
-                h_copies(1, lambda c: c.start())
-
-            @pl.when(j == 1)
-            def _():
-                h_copies(1, lambda c: c.wait())
+                for_rows(offset(cnt, l, loc, 4), lambda rows: h_copy(l, rows).wait())
 
         @pl.when(j + 1 < n2)
         def _():
@@ -298,15 +320,16 @@
             lax.fori_loop(0, 2, part, 0)
 
 
-def ffn(loc, cnt, tab, us, wd, *, pos=None, wg=None, wu=None, h_in=None):
+def ffn(loc, cnt, tab, us, wd, *, pos=None, wg=None, wu=None, h_in=None, xd=None, wq=None):
     n_tok, d = us[0].shape
     ff = wd.shape[1]
     nc = ff // FC
     n1 = 2 * nc if h_in is None else 0
+    n0 = 0 if n1 else wq.shape[1] // DC
     ns1 = 2
     once = lambda a: pl.BlockSpec(a.shape, lambda i, c: (0,) * a.ndim, pipeline_mode=pl.Buffered(1))
     hbm = pl.BlockSpec(memory_space=pl.ANY)
-    col = lambda i, c: (0, lax.div(jnp.maximum(i - n1, 0), 2))
+    col = lambda i, c: (0, lax.div(jnp.maximum(i - n1 - n0, 0), 2))
     scratch = [pltpu.VMEM((2, HALF, ff), BF16), pltpu.VMEM((2, HALF, DC), BF16), pltpu.VMEM((2, ff, DC), BF16),
                pltpu.VMEM((8, n_tok, SLOTS), BF16), pltpu.VMEM((12, n_tok, 128), F32), pltpu.SemaphoreType.DMA((2,))]
     if n1:
@@ -314,16 +337,19 @@
         specs = [once(tab), once(pos)] + [once(u) for u in us] + [hbm] * 3
         scratch += [pltpu.VMEM((2, HALF, d), BF16), pltpu.VMEM((ns1, d, 2 * FC), BF16), pltpu.SemaphoreType.DMA((ns1, 2))]
     else:
-        args = [tab, *us, h_in, wd]
-        specs = [once(tab)] + [pl.BlockSpec((n_tok, DC), col)] * 4 + [hbm] * 2
-        scratch += [pltpu.SemaphoreType.DMA((2,))]
-    out = jax.ShapeDtypeStruct((2 * n_tok, d), BF16)
-    out_spec = pl.BlockSpec((2 * n_tok, DC), col)
-    flops = (2 if h_in is not None else 6) * d * ff * 2 * HALF
-    return pl.pallas_call(
-        functools.partial(ffn_kernel, loc, n1, nc), out_shape=[out, out],
-        grid_spec=pltpu.PrefetchScalarGridSpec(num_scalar_prefetch=1, grid=(n1 + 2 * (d // DC),), in_specs=specs,
-                                               out_specs=[out_spec, out_spec], scratch_shapes=scratch),
+        args = [tab, *us, h_in, xd, wq, wd]
+        specs = [once(tab)] + [pl.BlockSpec((n_tok, DC), col)] * 4 + [hbm, once(xd), hbm, hbm]
+        scratch += [pltpu.VMEM((3, d, DC), BF16), pltpu.SemaphoreType.DMA((3,)), pltpu.SemaphoreType.DMA((2,))]
+    outs = [jax.ShapeDtypeStruct((2 * n_tok, d), BF16)] * 2
+    out_specs = [pl.BlockSpec((2 * n_tok, DC), col)] * 2
+    if n0:
+        outs.append(jax.ShapeDtypeStruct((n_tok, wq.shape[1]), BF16))
+        out_specs.append(pl.BlockSpec((n_tok, DC), lambda i, c: (0, jnp.minimum(i, n0 - 1))))
+    flops = (3 if h_in is not None else 6) * d * ff * 2 * HALF
+    return pl.pallas_call(
+        functools.partial(ffn_kernel, loc, n0, n1, nc), out_shape=outs,
+        grid_spec=pltpu.PrefetchScalarGridSpec(num_scalar_prefetch=1, grid=(n0 + n1 + 2 * (d // DC),), in_specs=specs,
+                                               out_specs=out_specs, scratch_shapes=scratch),
         compiler_params=pltpu.CompilerParams(vmem_limit_bytes=67043328),
         cost_estimate=pl.CostEstimate(flops=flops, bytes_accessed=flops // 512, transcendentals=0),
     )(cnt, *args)
@@ -337,34 +363,66 @@
     return [slice(c * 128, (c + 1) * 128) for c in range(width // 128)]
 
 
-def there_kernel(coef, u0, u1, keep, got, out):
-    n = u0.shape[0]
-    for mb, u in enumerate((u0, u1)):
-        r = slice(mb * n, (mb + 1) * n)
-        for c in lanes(u.shape[1]):
-            out[r, c] = lincomb(coef, 3 * mb, u[:, c], keep[r, c], got[r, c])
-
-
-def top_kernel(coef, u0, u1, keep, got, back, *outs):
-    n = u0.shape[0]
-    for mb, u in enumerate((u0, u1)):
-        r = slice(mb * n, (mb + 1) * n)
-        for c in lanes(u.shape[1]):
-            here = lincomb(coef, 6 * mb, u[:, c], keep[r, c], got[r, c])
-            outs[mb][:, c] = lincomb(coef, 6 * mb + 3, u[:, c], here, back[r, c])
-
-
-def mix(kernel, coef, us, rows, outs):
+def there_mix(coef, u, rows, mb, r, c):
+    keep, got = rows
+    return lincomb(coef, 3 * mb, u[:, c], keep[r, c], got[r, c])
+
+
+def top_mix(coef, u, rows, mb, r, c):
+    keep, got = rows[:2]
+    here = lincomb(coef, 6 * mb, u[:, c], keep[r, c], got[r, c])
+    return lincomb(coef, 6 * mb + 3, u[:, c], here, rows[2 + mb][:, c])
+
+
+def mix_kernel(fn, n_in, bw, coef, *refs):
+    srcs, outs = refs[:n_in], refs[n_in:n_in + 2]
+    dst, res, sem_i, sem_o = refs[n_in + 2:2 * n_in + 2], refs[2 * n_in + 2], refs[-2], refs[-1]
+    n, d = srcs[0].shape
+    steps = d // bw
+
+    def cut(c, start=0, width=bw):
+        return pl.ds(pl.multiple_of(c * bw + start, 128), width)
+
+    def loads(c):
+        return [pltpu.make_async_copy(s.at[:, cut(c)], t.at[:, cut(c)], sem_i.at[c, q])
+                for q, (s, t) in enumerate(zip(srcs, dst))]
+
+    def saves(c):
+        return [pltpu.make_async_copy(res.at[mb, :, cut(c)], outs[mb].at[:, cut(c)], sem_o.at[c, mb]) for mb in range(2)]
+
+    for c in range(steps):
+        for copy in loads(c):
+            copy.start()
+
+    def step(c, carry):
+        for copy in loads(c):
+            copy.wait()
+        for mb, save in enumerate(saves(c)):
+            for lane in lanes(bw):
+                cols = cut(c, lane.start, 128)
+                res[mb, :, cols] = fn(coef, dst[mb], dst[2:], mb, slice(mb * n, (mb + 1) * n), cols)
+            save.start()
+        return carry
+
+    lax.fori_loop(0, steps, step, 0)
+    for c in range(steps):
+        for copy in saves(c):
+            copy.wait()
+
+
+def mix(fn, coef, us, rows):
     n, d = us[0].shape
     bw = 384
-    at = lambda r: pl.BlockSpec((r, bw), lambda i: (0, i))
-    return pl.pallas_call(
-        kernel, out_shape=[jax.ShapeDtypeStruct((r, d), BF16) for r in outs], grid=(d // bw,),
-        in_specs=[pl.BlockSpec(coef.shape, lambda i: (0, 0, 0))] + [at(n)] * 2 + [at(2 * n)] * len(rows),
-        out_specs=[at(r) for r in outs],
+    srcs = [*us, *rows]
+    hbm = pl.BlockSpec(memory_space=pl.ANY)
+    return pl.pallas_call(
+        functools.partial(mix_kernel, fn, len(srcs), bw), out_shape=[jax.ShapeDtypeStruct((n, d), BF16)] * 2,
+        in_specs=[pl.BlockSpec(memory_space=pltpu.VMEM)] + [hbm] * len(srcs), out_specs=[hbm] * 2,
+        scratch_shapes=[pltpu.VMEM(a.shape, BF16) for a in srcs]
+        + [pltpu.VMEM((2, n, d), BF16), pltpu.SemaphoreType.DMA((d // bw, len(srcs))), pltpu.SemaphoreType.DMA((d // bw, 2))],
         compiler_params=pltpu.CompilerParams(vmem_limit_bytes=67043328),
         cost_estimate=pl.CostEstimate(flops=10 ** 9, bytes_accessed=10 ** 6, transcendentals=0),
-    )(coef, *us, *rows)
+    )(coef, *srcs)
 
 
 def dense_kernel(x, w, *refs):
@@ -389,7 +447,6 @@
 
 def solution(mesh):
     def layer(x_a, route_a, gate_a, h_b, attn_b, route_b, gate_b, w_qkv, w_o, w_gate, w_up, w_down):
-        n = x_a.shape[0]
         me = lax.axis_index('ep').astype(I32).reshape(1)
         meta = jnp.concatenate([route_a.T.astype(F32), route_b.T.astype(F32), gate_a.T, gate_b.T], axis=0)
         metas = [meta] + [swap(meta, k) for k in (1, 2, 3)]
@@ -404,12 +461,11 @@
         mid, top = spread(after(tab, h_loc))
         keep, send = ffn(1, after(cnt, mid), tab, (x_cnt, x_dia, b_cnt, b_dia), w_down, pos=pos, wg=w_gate, wu=w_up)
         got = swap(send, 1)
-        there, = mix(there_kernel, mid, (x_cnt, b_cnt), (keep, got), [2 * n])
-        back = swap(there, 2)
-        keep, send = ffn(0, after(cnt, there), tab, (x_a, x_par, mid_b, b_par), w_down, h_in=h_loc)
+        there = mix(there_mix, mid, (x_cnt, b_cnt), (keep, got))
+        back = [swap(t, 2) for t in there]
+        keep, send, qkv = ffn(0, after(cnt, there), tab, (x_a, x_par, mid_b, b_par), w_down, h_in=h_loc, xd=h_b, wq=w_qkv)
         got = swap(send, 1)
-        qkv = dense(after(h_b, keep), w_qkv, [])
-        out_a, out_b = mix(top_kernel, top, (x_a, mid_b), (keep, got, back), [n, n])
+        out_a, out_b = mix(top_mix, top, (x_a, mid_b), (keep, got, *back))
         return out_a, out_b, qkv
 
     row = P(('dp', 'ep'), None)

time: 310 us -> 322 us (1.039)
  waiting for transfers between devices: 43.9 us -> 59.4 us
  Pallas kernels: 202 us -> 195 us
  starting transfers between devices: 61.9 us -> 66 us
    pallas_call x2 -> x1, Pallas kernels: 25.4 us -> 7.86 us  [dense(): pl.pallas_call(dense_kernel, out_shape=jax.ShapeDtypeStruct((n, width), B...]
    ppermute x12 -> x13, waiting for transfers between devices: 43.9 us -> 59.4 us  [swap(): return lax.ppermute(x, 'ep', [(i, i ^ k) for i in range(N_SRC)])]
    pallas_call x4, Pallas kernels: 124 us -> 134 us  [the longest x2 121 us: ffn(): pl.pallas_call(functools.partial(ffn_kernel, loc, n0, n1, nc), out_shape=...]
    ppermute x12 -> x13, starting transfers between devices: 61.9 us -> 66 us  [swap(): return lax.ppermute(x, 'ep', [(i, i ^ k) for i in range(N_SRC)])]
  transfers between devices with their start and end apart: 12 -> 13, of which waited for: 6 -> 7; matrix products, arithmetic and copies ran while one was open for 0% -> 0% of each run, Pallas kernels for 23% -> 16%
where the time goes in v2:
time: 322 us
  Pallas kernels  195 us (61%)
  starting transfers between devices  66 us (20%)
  waiting for transfers between devices  59.4 us (18%)
    pallas_call x2, Pallas kernels, ffn(): pl.pallas_call(functools.partial(ffn_kernel, loc, n0, n1, nc), out_shape=...  121 us
    ppermute x13, starting transfers between devices, swap(): return lax.ppermute(x, 'ep', [(i, i ^ k) for i in range(N_SRC)])  66 us
    ppermute x13, waiting for transfers between devices, swap(): return lax.ppermute(x, 'ep', [(i, i ^ k) for i in range(N_SRC)])  59.4 us
    pallas_call x1, Pallas kernels, up(): pl.pallas_call(functools.partial(up_kernel, loc, ff // FC), out_shape=jax...  48.1 us
    pallas_call x2, Pallas kernels, mix(): pl.pallas_call(functools.partial(mix_kernel, fn, len(srcs), bw), out_shap...  13.2 us
    pallas_call x1, Pallas kernels, dense(): pl.pallas_call(dense_kernel, out_shape=jax.ShapeDtypeStruct((n, width), B...  7.86 us
  transfers between devices with their start and end apart: 13, of which 7 were waited for; matrix products, arithmetic and copies ran while one was open for 0% of the time, Pallas kernels for 16%

profile of v2, /device:TPU:0, one launch (start us, length us, event | category | flops | bytes accessed | tf_op | source)
XLA Modules:
  0.0 321.7 jit_solution(4888756239953419810)
XLA Ops:
  0.7 7.9 %shard_map.139.ub0.refs_2_.refs_1_ = bf16[256,2304]{1,0:T(8,128)(2,1)} custom-call(bf16[256,2304]{1,0:T(8,128)(2,1)} %x.1, bf16[2304,2304]{1,0:T(8,128)(2,1)} %w.1, bf16[256,2304]{1,0:T(8,128)(2,1)} %refs_5_.3), custom_call_target="tpu_custom_call" | custom-call | flops 2717908992 | bytes 10616832 | tf_op jit(solution)/shard_map/pallas_call | solution.py:439
  8.5 0.8 collective-permute-start.4
  9.4 0.0 copy-start
  9.4 2.6 collective-permute-start.2
  12.1 0.4 collective-permute-start.1
  12.5 0.1 collective-permute-start
  12.6 0.9 collective-permute-done.2.m3
  13.4 2.1 collective-permute-start.6
  15.5 0.2 collective-permute-done.1.m2
  15.7 0.4 collective-permute-start.5
  16.1 0.0 collective-permute-done.m1
  16.1 0.2 copy-done.2
  16.3 0.4 copy-done.3
  16.7 1.8 route.1
  18.5 48.1 %shard_map.140.refs_4_ = bf16[2,512,5760]{2,1,0:T(8,128)(2,1)} custom-call(s32[2,8,128]{2,1,0:T(8,128)} %get-tuple-element.35.cnt, f32[2,8,256]{2,1,0:T(8,128)} %get-tuple-element.24.pos.refs_0_, bf16[256,2304]{1,0:T(8,128)(2,1)} %refs_0_.5, bf16[256,2304]{1,0:T(8,128)(2,1)} %collective-permute-done.3.ua1.refs_1_, ...), custom_call_target="tpu_custom_call" | custom-call | flops 54358179840 | bytes 106168320 | tf_op jit(solution)/shard_map/pallas_call | solution.py:188
  66.6 0.7 collective-permute-done.5.refs_1_.refs_0_
  67.4 18.5 %collective-permute-start.7 = (bf16[256,2304]{1,0:T(8,128)(2,1)}, bf16[256,2304]{1,0:T(8,128)(2,1)}, u32[]{:S(2)}, u32[]{:S(2)}) collective-permute-start(bf16[256,2304]{1,0:T(8,128)(2,1)} %collective-permute-done.5.refs_1_.refs_0_), channel_id=1, source_target_pairs={{0,1},{1,0},{2,3},{3,2},{4,5},{5,4},{6,7},{7,6}} | collective-permute-start | bytes 3538952 | tf_op jit(solution)/shard_map/ppermute | solution.py:23
  85.8 0.0 collective-permute-start.8
  85.9 2.9 spread.1
  88.8 0.0 collective-permute-done.7.refs_2_
  88.8 1.6 collective-permute-done.8.refs_4_
  90.4 74.0 %shard_map.141 = (bf16[512,2304]{1,0:T(8,128)(2,1)}, bf16[512,2304]{1,0:T(8,128)(2,1)}) custom-call(s32[2,8,128]{2,1,0:T(8,128)} %get-tuple-element.35.cnt, f32[2,256,128]{2,1,0:T(8,128)} %get-tuple-element.25.tab, f32[2,8,256]{2,1,0:T(8,128)} %get-tuple-element.24.pos.refs_0_, bf16[256,2304]{1,0:T(8,128)(2,1)} %collective-permute-done.5.refs_1_.refs_0_, ...), custom_call_target="tpu_custom_call" | custom-call | flops 81537269760 | bytes 159252480 | tf_op jit(solution)/shard_map/pallas_call | solution.py:349
  164.4 29.3 %collective-permute-start.9 = (bf16[512,2304]{1,0:T(8,128)(2,1)}, bf16[512,2304]{1,0:T(8,128)(2,1)}, u32[]{:S(2)}, u32[]{:S(2)}) collective-permute-start(bf16[512,2304]{1,0:T(8,128)(2,1)} %get-tuple-element.32), channel_id=1, source_target_pairs={{0,1},{1,0},{2,3},{3,2},{4,5},{5,4},{6,7},{7,6}} | collective-permute-start | bytes 7077896 | tf_op jit(solution)/shard_map/ppermute | solution.py:23
  193.8 4.5 %collective-permute-done.9.refs_3_ = bf16[512,2304]{1,0:T(8,128)(2,1)} collective-permute-done((bf16[512,2304]{1,0:T(8,128)(2,1)}, bf16[512,2304]{1,0:T(8,128)(2,1)}, u32[]{:S(2)}, u32[]{:S(2)}) %collective-permute-start.9) | collective-permute-done | bytes 2359328 | tf_op jit(solution)/shard_map/ppermute | solution.py:23
  198.3 5.9 %shard_map.142 = (bf16[256,2304]{1,0:T(8,128)(2,1)}, bf16[256,2304]{1,0:T(8,128)(2,1)}) custom-call(f32[6,256,128]{2,1,0:T(8,128)} %get-tuple-element.27.coef, bf16[256,2304]{1,0:T(8,128)(2,1)} %collective-permute-done.5.refs_1_.refs_0_, bf16[256,2304]{1,0:T(8,128)(2,1)} %collective-permute-done.6.refs_3_.refs_1_, ...), custom_call_target="tpu_custom_call" | custom-call | flops 1000000000 | bytes 1000000 | tf_op jit(solution)/shard_map/pallas_call | solution.py:418
  204.2 46.9 %shard_map.143 = (bf16[512,2304]{1,0:T(8,128)(2,1)}, bf16[512,2304]{1,0:T(8,128)(2,1)}, bf16[256,6912]{1,0:T(8,128)(2,1)}) custom-call(s32[2,8,128]{2,1,0:T(8,128)} %get-tuple-element.35.cnt, f32[2,256,128]{2,1,0:T(8,128)} %get-tuple-element.25.tab, bf16[256,2304]{1,0:T(8,128)(2,1)} %refs_0_.5, bf16[256,2304]{1,0:T(8,128)(2,1)} %collective-permute-done.3.ua1.refs_1_, ...), custom_call_target="tpu_custom_call" | custom-call | flops 40768634880 | bytes 79626240 | tf_op jit(solution)/shard_map/pallas_call | solution.py:349
  251.1 9.6 %collective-permute-start.10 = (bf16[512,2304]{1,0:T(8,128)(2,1)}, bf16[512,2304]{1,0:T(8,128)(2,1)}, u32[]{:S(2)}, u32[]{:S(2)}) collective-permute-start(bf16[512,2304]{1,0:T(8,128)(2,1)} %get-tuple-element.37), channel_id=1, source_target_pairs={{0,1},{1,0},{2,3},{3,2},{4,5},{5,4},{6,7},{7,6}} | collective-permute-start | bytes 7077896 | tf_op jit(solution)/shard_map/ppermute | solution.py:23
  260.7 0.0 collective-permute-start.11
  260.8 2.0 collective-permute-start.12
  262.8 27.1 %collective-permute-done.11.refs_4_ = bf16[256,2304]{1,0:T(8,128)(2,1)} collective-permute-done((bf16[256,2304]{1,0:T(8,128)(2,1)}, bf16[256,2304]{1,0:T(8,128)(2,1)}, u32[]{:S(2)}, u32[]{:S(2)}) %collective-permute-start.11) | collective-permute-done | bytes 1179680 | tf_op jit(solution)/shard_map/ppermute | solution.py:23
  289.9 24.3 %collective-permute-done.12.refs_5_ = bf16[256,2304]{1,0:T(8,128)(2,1)} collective-permute-done((bf16[256,2304]{1,0:T(8,128)(2,1)}, bf16[256,2304]{1,0:T(8,128)(2,1)}, u32[]{:S(2)}, u32[]{:S(2)}) %collective-permute-start.12) | collective-permute-done | bytes 1179680 | tf_op jit(solution)/shard_map/ppermute | solution.py:23
  314.3 7.3 %shard_map.144 = (bf16[256,2304]{1,0:T(8,128)(2,1)}, bf16[256,2304]{1,0:T(8,128)(2,1)}) custom-call(f32[12,256,128]{2,1,0:T(8,128)} %get-tuple-element.26.coef, bf16[256,2304]{1,0:T(8,128)(2,1)} %refs_0_.5, bf16[256,2304]{1,0:T(8,128)(2,1)} %shard_map.139.ub0.refs_2_.refs_1_, bf16[512,2304]{1,0:T(8,128)(2,1)} %get-tuple-element.36.refs_2_, ...), custom_call_target="tpu_custom_call" | custom-call | flops 1000000000 | bytes 1000000 | tf_op jit(solution)/shard_map/pallas_call | solution.py:418
  (20 shorter events, 0.1 us)
Async XLA Ops:
  0.6 8.7 %copy-start.4 = (s32[256,2]{0,1:T(2,128)S(1)}, s32[256,2]{0,1:T(2,128)}, u32[]{:S(2)}) copy-start(s32[256,2]{0,1:T(2,128)} %param.17) | copy-start | bytes 6148
  0.6 8.7 %copy-start.5 = (s32[256,2]{0,1:T(2,128)S(1)}, s32[256,2]{0,1:T(2,128)}, u32[]{:S(2)}) copy-start(s32[256,2]{0,1:T(2,128)} %param.13) | copy-start | bytes 6148
  0.7 8.7 %copy-start.6 = (f32[256,2]{0,1:T(2,128)S(1)}, f32[256,2]{0,1:T(2,128)}, u32[]{:S(2)}) copy-start(f32[256,2]{0,1:T(2,128)} %param.18) | copy-start | bytes 6148
  0.7 8.7 %copy-start.7 = (f32[256,2]{0,1:T(2,128)S(1)}, f32[256,2]{0,1:T(2,128)}, u32[]{:S(2)}) copy-start(f32[256,2]{0,1:T(2,128)} %param.14) | copy-start | bytes 6148
  8.5 10.0 %collective-permute-start.4 = (bf16[256,2304]{1,0:T(8,128)(2,1)}, bf16[256,2304]{1,0:T(8,128)(2,1)}, u32[]{:S(2)}, u32[]{:S(2)}) collective-permute-start(bf16[256,2304]{1,0:T(8,128)(2,1)} %shard_map.139.ub0.refs_2_.refs_1_), channel_id=1, source_target_pairs={{0,1},{1,0},{2,3},{3,2},{4,5},{5,4},{6,7},{7,6}} | collective-permute-start | bytes 3538952 | tf_op jit(solution)/shard_map/ppermute | solution.py:23
  9.4 9.1 %collective-permute-start.3 = (bf16[256,2304]{1,0:T(8,128)(2,1)}, bf16[256,2304]{1,0:T(8,128)(2,1)}, u32[]{:S(2)}, u32[]{:S(2)}) collective-permute-start(bf16[256,2304]{1,0:T(8,128)(2,1)} %refs_0_.5), channel_id=1, source_target_pairs={{0,1},{1,0},{2,3},{3,2},{4,5},{5,4},{6,7},{7,6}} | collective-permute-start | bytes 3538952 | tf_op jit(solution)/shard_map/ppermute | solution.py:23
  9.4 6.7 %copy-start = (f32[8,256]{1,0:T(8,128)}, f32[8,256]{1,0:T(8,128)S(1)}, u32[]{:S(2)}) copy-start(f32[8,256]{1,0:T(8,128)S(1)} %pad_maximum_fusion.m0) | copy-start | bytes 24580
  9.4 4.0 %collective-permute-start.2 = (f32[8,256]{1,0:T(8,128)S(1)}, f32[8,256]{1,0:T(8,128)S(1)}, u32[]{:S(2)}, u32[]{:S(2)}) collective-permute-start(f32[8,256]{1,0:T(8,128)S(1)} %pad_maximum_fusion.m0), channel_id=1, source_target_pairs={{0,3},{1,2},{2,1},{3,0},{4,7},{5,6},{6,5},{7,4}} | collective-permute-start | bytes 24584 | tf_op jit(solution)/shard_map/ppermute | solution.py:23
  12.1 3.7 %collective-permute-start.1 = (f32[8,256]{1,0:T(8,128)S(1)}, f32[8,256]{1,0:T(8,128)S(1)}, u32[]{:S(2)}, u32[]{:S(2)}) collective-permute-start(f32[8,256]{1,0:T(8,128)S(1)} %pad_maximum_fusion.m0), channel_id=1, source_target_pairs={{0,2},{1,3},{2,0},{3,1},{4,6},{5,7},{6,4},{7,5}} | collective-permute-start | bytes 24584 | tf_op jit(solution)/shard_map/ppermute | solution.py:23
  12.5 3.7 %collective-permute-start = (f32[8,256]{1,0:T(8,128)S(1)}, f32[8,256]{1,0:T(8,128)S(1)}, u32[]{:S(2)}, u32[]{:S(2)}) collective-permute-start(f32[8,256]{1,0:T(8,128)S(1)} %pad_maximum_fusion.m0), channel_id=1, source_target_pairs={{0,1},{1,0},{2,3},{3,2},{4,5},{5,4},{6,7},{7,6}} | collective-permute-start | bytes 24584 | tf_op jit(solution)/shard_map/ppermute | solution.py:23
  13.4 2.7 copy-start.1
  13.4 53.2 %collective-permute-start.6 = (bf16[256,2304]{1,0:T(8,128)(2,1)}, bf16[256,2304]{1,0:T(8,128)(2,1)}, u32[]{:S(2)}, u32[]{:S(2)}) collective-permute-start(bf16[256,2304]{1,0:T(8,128)(2,1)} %shard_map.139.ub0.refs_2_.refs_1_), channel_id=1, source_target_pairs={{0,2},{1,3},{2,0},{3,1},{4,6},{5,7},{6,4},{7,5}} | collective-permute-start | bytes 3538952 | tf_op jit(solution)/shard_map/ppermute | solution.py:23
  15.7 0.6 copy-start.2
  15.7 51.7 %collective-permute-start.5 = (bf16[256,2304]{1,0:T(8,128)(2,1)}, bf16[256,2304]{1,0:T(8,128)(2,1)}, u32[]{:S(2)}, u32[]{:S(2)}) collective-permute-start(bf16[256,2304]{1,0:T(8,128)(2,1)} %refs_0_.5), channel_id=1, source_target_pairs={{0,2},{1,3},{2,0},{3,1},{4,6},{5,7},{6,4},{7,5}} | collective-permute-start | bytes 3538952 | tf_op jit(solution)/shard_map/ppermute | solution.py:23
  16.1 0.6 copy-start.3
  67.4 21.4 %collective-permute-start.7 = (bf16[256,2304]{1,0:T(8,128)(2,1)}, bf16[256,2304]{1,0:T(8,128)(2,1)}, u32[]{:S(2)}, u32[]{:S(2)}) collective-permute-start(bf16[256,2304]{1,0:T(8,128)(2,1)} %collective-permute-done.5.refs_1_.refs_0_), channel_id=1, source_target_pairs={{0,1},{1,0},{2,3},{3,2},{4,5},{5,4},{6,7},{7,6}} | collective-permute-start | bytes 3538952 | tf_op jit(solution)/shard_map/ppermute | solution.py:23
  85.8 4.5 %collective-permute-start.8 = (bf16[256,2304]{1,0:T(8,128)(2,1)}, bf16[256,2304]{1,0:T(8,128)(2,1)}, u32[]{:S(2)}, u32[]{:S(2)}) collective-permute-start(bf16[256,2304]{1,0:T(8,128)(2,1)} %collective-permute-done.6.refs_3_.refs_1_), channel_id=1, source_target_pairs={{0,1},{1,0},{2,3},{3,2},{4,5},{5,4},{6,7},{7,6}} | collective-permute-start | bytes 3538952 | tf_op jit(solution)/shard_map/ppermute | solution.py:23
  164.4 33.9 %collective-permute-start.9 = (bf16[512,2304]{1,0:T(8,128)(2,1)}, bf16[512,2304]{1,0:T(8,128)(2,1)}, u32[]{:S(2)}, u32[]{:S(2)}) collective-permute-start(bf16[512,2304]{1,0:T(8,128)(2,1)} %get-tuple-element.32), channel_id=1, source_target_pairs={{0,1},{1,0},{2,3},{3,2},{4,5},{5,4},{6,7},{7,6}} | collective-permute-start | bytes 7077896 | tf_op jit(solution)/shard_map/ppermute | solution.py:23
  251.1 63.1 %collective-permute-start.10 = (bf16[512,2304]{1,0:T(8,128)(2,1)}, bf16[512,2304]{1,0:T(8,128)(2,1)}, u32[]{:S(2)}, u32[]{:S(2)}) collective-permute-start(bf16[512,2304]{1,0:T(8,128)(2,1)} %get-tuple-element.37), channel_id=1, source_target_pairs={{0,1},{1,0},{2,3},{3,2},{4,5},{5,4},{6,7},{7,6}} | collective-permute-start | bytes 7077896 | tf_op jit(solution)/shard_map/ppermute | solution.py:23
  260.7 29.2 %collective-permute-start.11 = (bf16[256,2304]{1,0:T(8,128)(2,1)}, bf16[256,2304]{1,0:T(8,128)(2,1)}, u32[]{:S(2)}, u32[]{:S(2)}) collective-permute-start(bf16[256,2304]{1,0:T(8,128)(2,1)} %get-tuple-element.33), channel_id=1, source_target_pairs={{0,2},{1,3},{2,0},{3,1},{4,6},{5,7},{6,4},{7,5}} | collective-permute-start | bytes 3538952 | tf_op jit(solution)/shard_map/ppermute | solution.py:23
  260.8 53.5 %collective-permute-start.12 = (bf16[256,2304]{1,0:T(8,128)(2,1)}, bf16[256,2304]{1,0:T(8,128)(2,1)}, u32[]{:S(2)}, u32[]{:S(2)}) collective-permute-start(bf16[256,2304]{1,0:T(8,128)(2,1)} %get-tuple-element.34), channel_id=1, source_target_pairs={{0,2},{1,3},{2,0},{3,1},{4,6},{5,7},{6,4},{7,5}} | collective-permute-start | bytes 3538952 | tf_op jit(solution)/shard_map/ppermute | solution.py:23

commit v3 on v2

--- a/solution.py
+++ b/solution.py
@@ -12,7 +12,8 @@
 N_SRC = 4
 SLOTS = 128
 HALF = 512
-VARIANTS = (256, 384, 512)
+UP_ROWS = (320, 384, 448, 512)
+DOWN_ROWS = ((384, 512), (384, 448, 512))
 FC, DC = 640, 768
 MIB = 2 ** 20
 
@@ -117,9 +118,9 @@
     return off
 
 
-def for_rows(m, body):
+def for_rows(variants, m, body):
     lo = 0
-    for rows in VARIANTS:
+    for rows in variants:
         pl.when(jnp.logical_and(m > lo, m <= rows))(functools.partial(body, rows))
         lo = rows
 
@@ -133,25 +134,20 @@
         return [pltpu.make_async_copy(wg.at[l, :, cols], w.at[s, :, pl.ds(0, FC)], sem.at[s, 0]),
                 pltpu.make_async_copy(wu.at[l, :, cols], w.at[s, :, pl.ds(FC, FC)], sem.at[s, 1])]
 
-    def gather(l):
-        x[l] = jnp.zeros(x.shape[1:], BF16)
-        for k in range(4):
-            q = l * N_SRC + 2 * loc + k % 2
-            p = pos[k // 2, q:q + 1, :]
-            pick = (lax.broadcasted_iota(I32, (SLOTS, p.shape[1]), 0).astype(F32) == p).astype(BF16)
-            rows = jnp.dot(pick, us[k][...], preferred_element_type=F32)
-            x[l, pl.ds(pl.multiple_of(offset(cnt, l, loc, k), 16), SLOTS), :] = rows.astype(BF16)
-
     @pl.when(i == 0)
     def _():
         for j in range(ns - 1):
             for c in copies(j):
                 c.start()
-        gather(0)
-
-    @pl.when(i == 1)
-    def _():
-        gather(1)
+
+    @pl.when(i < 2)
+    def _():
+        x[i] = jnp.zeros(x.shape[1:], BF16)
+        for k in range(4):
+            p = pos[k // 2, pl.ds(i * N_SRC + 2 * loc + k % 2, 1), :]
+            pick = (lax.broadcasted_iota(I32, (SLOTS, p.shape[1]), 0).astype(F32) == p).astype(BF16)
+            rows = jnp.dot(pick, us[k][...], preferred_element_type=F32)
+            x[i, pl.ds(pl.multiple_of(offset(cnt, i, loc, k), 16), SLOTS), :] = rows.astype(BF16)
 
     @pl.when(i + ns - 1 < n)
     def _():
@@ -168,12 +164,17 @@
         def body(rows):
             r = jnp.dot(x[l, :rows], w[s], preferred_element_type=F32)
             res = (jax.nn.silu(r[:, :FC]) * r[:, FC:]).astype(BF16)
+            rest = jnp.zeros((HALF - rows, FC), BF16)
             if whole:
                 h[l, :rows, cols] = res
+                if rows < HALF:
+                    h[l, rows:, cols] = rest
             else:
                 h[0, :rows] = res
-
-        for_rows(offset(cnt, l, loc, 4), body)
+                if rows < HALF:
+                    h[0, rows:] = rest
+
+        for_rows(UP_ROWS, offset(cnt, l, loc, 4), body)
 
 
 def up_kernel(loc, nc, cnt, pos, ua0, ua1, ub0, ub1, wg, wu, h, x, w, sem):
@@ -222,7 +223,7 @@
         return pltpu.make_async_copy(h_in.at[e, pl.ds(0, rows)], h.at[e, pl.ds(0, rows)], sh.at[e])
 
     def h_copies(e, act):
-        for_rows(offset(cnt, e, loc, 4), lambda rows: act(h_copy(e, rows)))
+        for_rows(DOWN_ROWS[loc], offset(cnt, e, loc, 4), lambda rows: act(h_copy(e, rows)))
 
     if not n1:
         def copy0(j):
@@ -283,7 +284,7 @@
         if not n1:
             @pl.when(j < 2)
             def _():
-                for_rows(offset(cnt, l, loc, 4), lambda rows: h_copy(l, rows).wait())
+                for_rows(DOWN_ROWS[loc], offset(cnt, l, loc, 4), lambda rows: h_copy(l, rows).wait())
 
         @pl.when(j + 1 < n2)
         def _():
@@ -294,7 +295,7 @@
         def body(rows):
             y[l, :rows] = jnp.dot(h[l, :rows], w2[l], preferred_element_type=F32).astype(BF16)
 
-        for_rows(offset(cnt, l, loc, 4), body)
+        for_rows(DOWN_ROWS[loc], offset(cnt, l, loc, 4), body)
 
         @pl.when(l == 1)
         def _():

time: 322 us -> 321 us (level)
  starting transfers between devices: 66 us -> 54.2 us
  Pallas kernels: 195 us -> 206 us
    ppermute x13, starting transfers between devices: 66 us -> 54.2 us  [swap(): return lax.ppermute(x, 'ep', [(i, i ^ k) for i in range(N_SRC)])]
    pallas_call x2, Pallas kernels: 121 us -> 130 us  [ffn(): pl.pallas_call(functools.partial(ffn_kernel, loc, n0, n1, nc), out_shape=...]
  transfers between devices with their start and end apart: 13 -> 13, of which waited for: 7 -> 6; matrix products, arithmetic and copies ran while one was open for 0% -> 0% of each run, Pallas kernels for 16% -> 17%
where the time goes in v3:
time: 321 us; the launch traced here: 320 us
  Pallas kernels  206 us (64%)
  waiting for transfers between devices  58.6 us (18%)
  starting transfers between devices  54.2 us (17%)
    pallas_call x2, Pallas kernels, ffn(): pl.pallas_call(functools.partial(ffn_kernel, loc, n0, n1, nc), out_shape=...  130 us
    ppermute x13, waiting for transfers between devices, swap(): return lax.ppermute(x, 'ep', [(i, i ^ k) for i in range(N_SRC)])  58.6 us
    ppermute x13, starting transfers between devices, swap(): return lax.ppermute(x, 'ep', [(i, i ^ k) for i in range(N_SRC)])  54.2 us
    pallas_call x1, Pallas kernels, up(): pl.pallas_call(functools.partial(up_kernel, loc, ff // FC), out_shape=jax...  50.7 us
    pallas_call x2, Pallas kernels, mix(): pl.pallas_call(functools.partial(mix_kernel, fn, len(srcs), bw), out_shap...  13.2 us
    pallas_call x1, Pallas kernels, dense(): pl.pallas_call(dense_kernel, out_shape=jax.ShapeDtypeStruct((n, width), B...  7.86 us
  transfers between devices with their start and end apart: 13, of which 6 were waited for; matrix products, arithmetic and copies ran while one was open for 0% of the time, Pallas kernels for 17%

profile of v3, /device:TPU:0, one launch (start us, length us, event | category | flops | bytes accessed | tf_op | source)
XLA Modules:
  0.0 320.3 jit_solution(10804826728491002656)
XLA Ops:
  0.7 7.9 %shard_map.139.ub0.refs_2_.refs_1_ = bf16[256,2304]{1,0:T(8,128)(2,1)} custom-call(bf16[256,2304]{1,0:T(8,128)(2,1)} %x.1, bf16[2304,2304]{1,0:T(8,128)(2,1)} %w.1, bf16[256,2304]{1,0:T(8,128)(2,1)} %refs_5_.3), custom_call_target="tpu_custom_call" | custom-call | flops 2717908992 | bytes 10616832 | tf_op jit(solution)/shard_map/pallas_call | solution.py:440
  8.5 0.8 collective-permute-start.4
  9.4 0.0 copy-start
  9.4 2.6 collective-permute-start.2
  12.1 0.4 collective-permute-start.1
  12.5 0.1 collective-permute-start
  12.6 0.9 collective-permute-done.2.m3
  13.4 2.1 collective-permute-start.6
  15.5 0.2 collective-permute-done.1.m2
  15.7 0.4 collective-permute-start.5
  16.1 0.0 collective-permute-done.m1
  16.1 0.2 copy-done.2
  16.3 0.4 copy-done.3
  16.7 1.8 route.1
  18.5 50.7 %shard_map.140.refs_4_ = bf16[2,512,5760]{2,1,0:T(8,128)(2,1)} custom-call(s32[2,8,128]{2,1,0:T(8,128)} %get-tuple-element.35.cnt, f32[2,8,256]{2,1,0:T(8,128)} %get-tuple-element.24.pos.refs_0_, bf16[256,2304]{1,0:T(8,128)(2,1)} %refs_0_.5, bf16[256,2304]{1,0:T(8,128)(2,1)} %collective-permute-done.3.ua1.refs_1_, ...), custom_call_target="tpu_custom_call" | custom-call | flops 54358179840 | bytes 106168320 | tf_op jit(solution)/shard_map/pallas_call | solution.py:189
  69.2 0.0 collective-permute-done.5.refs_1_.refs_0_
  69.2 16.1 %collective-permute-start.7 = (bf16[256,2304]{1,0:T(8,128)(2,1)}, bf16[256,2304]{1,0:T(8,128)(2,1)}, u32[]{:S(2)}, u32[]{:S(2)}) collective-permute-start(bf16[256,2304]{1,0:T(8,128)(2,1)} %collective-permute-done.5.refs_1_.refs_0_), channel_id=1, source_target_pairs={{0,1},{1,0},{2,3},{3,2},{4,5},{5,4},{6,7},{7,6}} | collective-permute-start | bytes 3538952 | tf_op jit(solution)/shard_map/ppermute | solution.py:24
  85.3 0.0 collective-permute-start.8
  85.4 2.9 spread.1
  88.2 0.0 collective-permute-done.7.refs_2_
  88.2 1.6 collective-permute-done.8.refs_4_
  89.8 81.0 %shard_map.141 = (bf16[512,2304]{1,0:T(8,128)(2,1)}, bf16[512,2304]{1,0:T(8,128)(2,1)}) custom-call(s32[2,8,128]{2,1,0:T(8,128)} %get-tuple-element.35.cnt, f32[2,256,128]{2,1,0:T(8,128)} %get-tuple-element.25.tab, f32[2,8,256]{2,1,0:T(8,128)} %get-tuple-element.24.pos.refs_0_, bf16[256,2304]{1,0:T(8,128)(2,1)} %collective-permute-done.5.refs_1_.refs_0_, ...), custom_call_target="tpu_custom_call" | custom-call | flops 81537269760 | bytes 159252480 | tf_op jit(solution)/shard_map/pallas_call | solution.py:350
  170.9 21.6 %collective-permute-start.9 = (bf16[512,2304]{1,0:T(8,128)(2,1)}, bf16[512,2304]{1,0:T(8,128)(2,1)}, u32[]{:S(2)}, u32[]{:S(2)}) collective-permute-start(bf16[512,2304]{1,0:T(8,128)(2,1)} %get-tuple-element.32), channel_id=1, source_target_pairs={{0,1},{1,0},{2,3},{3,2},{4,5},{5,4},{6,7},{7,6}} | collective-permute-start | bytes 7077896 | tf_op jit(solution)/shard_map/ppermute | solution.py:24
  192.4 4.5 %collective-permute-done.9.refs_3_ = bf16[512,2304]{1,0:T(8,128)(2,1)} collective-permute-done((bf16[512,2304]{1,0:T(8,128)(2,1)}, bf16[512,2304]{1,0:T(8,128)(2,1)}, u32[]{:S(2)}, u32[]{:S(2)}) %collective-permute-start.9) | collective-permute-done | bytes 2359328 | tf_op jit(solution)/shard_map/ppermute | solution.py:24
  197.0 5.9 %shard_map.142 = (bf16[256,2304]{1,0:T(8,128)(2,1)}, bf16[256,2304]{1,0:T(8,128)(2,1)}) custom-call(f32[6,256,128]{2,1,0:T(8,128)} %get-tuple-element.27.coef, bf16[256,2304]{1,0:T(8,128)(2,1)} %collective-permute-done.5.refs_1_.refs_0_, bf16[256,2304]{1,0:T(8,128)(2,1)} %collective-permute-done.6.refs_3_.refs_1_, ...), custom_call_target="tpu_custom_call" | custom-call | flops 1000000000 | bytes 1000000 | tf_op jit(solution)/shard_map/pallas_call | solution.py:419
  202.9 48.5 %shard_map.143 = (bf16[512,2304]{1,0:T(8,128)(2,1)}, bf16[512,2304]{1,0:T(8,128)(2,1)}, bf16[256,6912]{1,0:T(8,128)(2,1)}) custom-call(s32[2,8,128]{2,1,0:T(8,128)} %get-tuple-element.35.cnt, f32[2,256,128]{2,1,0:T(8,128)} %get-tuple-element.25.tab, bf16[256,2304]{1,0:T(8,128)(2,1)} %refs_0_.5, bf16[256,2304]{1,0:T(8,128)(2,1)} %collective-permute-done.3.ua1.refs_1_, ...), custom_call_target="tpu_custom_call" | custom-call | flops 40768634880 | bytes 79626240 | tf_op jit(solution)/shard_map/pallas_call | solution.py:350
  251.4 8.0 %collective-permute-start.10 = (bf16[512,2304]{1,0:T(8,128)(2,1)}, bf16[512,2304]{1,0:T(8,128)(2,1)}, u32[]{:S(2)}, u32[]{:S(2)}) collective-permute-start(bf16[512,2304]{1,0:T(8,128)(2,1)} %get-tuple-element.37), channel_id=1, source_target_pairs={{0,1},{1,0},{2,3},{3,2},{4,5},{5,4},{6,7},{7,6}} | collective-permute-start | bytes 7077896 | tf_op jit(solution)/shard_map/ppermute | solution.py:24
  259.4 0.0 collective-permute-start.11
  259.4 2.0 collective-permute-start.12
  261.4 27.1 %collective-permute-done.11.refs_4_ = bf16[256,2304]{1,0:T(8,128)(2,1)} collective-permute-done((bf16[256,2304]{1,0:T(8,128)(2,1)}, bf16[256,2304]{1,0:T(8,128)(2,1)}, u32[]{:S(2)}, u32[]{:S(2)}) %collective-permute-start.11) | collective-permute-done | bytes 1179680 | tf_op jit(solution)/shard_map/ppermute | solution.py:24
  288.5 24.3 %collective-permute-done.12.refs_5_ = bf16[256,2304]{1,0:T(8,128)(2,1)} collective-permute-done((bf16[256,2304]{1,0:T(8,128)(2,1)}, bf16[256,2304]{1,0:T(8,128)(2,1)}, u32[]{:S(2)}, u32[]{:S(2)}) %collective-permute-start.12) | collective-permute-done | bytes 1179680 | tf_op jit(solution)/shard_map/ppermute | solution.py:24
  312.9 7.3 %shard_map.144 = (bf16[256,2304]{1,0:T(8,128)(2,1)}, bf16[256,2304]{1,0:T(8,128)(2,1)}) custom-call(f32[12,256,128]{2,1,0:T(8,128)} %get-tuple-element.26.coef, bf16[256,2304]{1,0:T(8,128)(2,1)} %refs_0_.5, bf16[256,2304]{1,0:T(8,128)(2,1)} %shard_map.139.ub0.refs_2_.refs_1_, bf16[512,2304]{1,0:T(8,128)(2,1)} %get-tuple-element.36.refs_2_, ...), custom_call_target="tpu_custom_call" | custom-call | flops 1000000000 | bytes 1000000 | tf_op jit(solution)/shard_map/pallas_call | solution.py:419
  (20 shorter events, 0.1 us)
Async XLA Ops:
  0.6 8.7 %copy-start.4 = (s32[256,2]{0,1:T(2,128)S(1)}, s32[256,2]{0,1:T(2,128)}, u32[]{:S(2)}) copy-start(s32[256,2]{0,1:T(2,128)} %param.17) | copy-start | bytes 6148
  0.6 8.7 %copy-start.5 = (s32[256,2]{0,1:T(2,128)S(1)}, s32[256,2]{0,1:T(2,128)}, u32[]{:S(2)}) copy-start(s32[256,2]{0,1:T(2,128)} %param.13) | copy-start | bytes 6148
  0.7 8.7 %copy-start.6 = (f32[256,2]{0,1:T(2,128)S(1)}, f32[256,2]{0,1:T(2,128)}, u32[]{:S(2)}) copy-start(f32[256,2]{0,1:T(2,128)} %param.18) | copy-start | bytes 6148
  0.7 8.7 %copy-start.7 = (f32[256,2]{0,1:T(2,128)S(1)}, f32[256,2]{0,1:T(2,128)}, u32[]{:S(2)}) copy-start(f32[256,2]{0,1:T(2,128)} %param.14) | copy-start | bytes 6148
  8.5 10.0 %collective-permute-start.4 = (bf16[256,2304]{1,0:T(8,128)(2,1)}, bf16[256,2304]{1,0:T(8,128)(2,1)}, u32[]{:S(2)}, u32[]{:S(2)}) collective-permute-start(bf16[256,2304]{1,0:T(8,128)(2,1)} %shard_map.139.ub0.refs_2_.refs_1_), channel_id=1, source_target_pairs={{0,1},{1,0},{2,3},{3,2},{4,5},{5,4},{6,7},{7,6}} | collective-permute-start | bytes 3538952 | tf_op jit(solution)/shard_map/ppermute | solution.py:24
  9.4 9.1 %collective-permute-start.3 = (bf16[256,2304]{1,0:T(8,128)(2,1)}, bf16[256,2304]{1,0:T(8,128)(2,1)}, u32[]{:S(2)}, u32[]{:S(2)}) collective-permute-start(bf16[256,2304]{1,0:T(8,128)(2,1)} %refs_0_.5), channel_id=1, source_target_pairs={{0,1},{1,0},{2,3},{3,2},{4,5},{5,4},{6,7},{7,6}} | collective-permute-start | bytes 3538952 | tf_op jit(solution)/shard_map/ppermute | solution.py:24
  9.4 6.7 %copy-start = (f32[8,256]{1,0:T(8,128)}, f32[8,256]{1,0:T(8,128)S(1)}, u32[]{:S(2)}) copy-start(f32[8,256]{1,0:T(8,128)S(1)} %pad_maximum_fusion.m0) | copy-start | bytes 24580
  9.4 4.0 %collective-permute-start.2 = (f32[8,256]{1,0:T(8,128)S(1)}, f32[8,256]{1,0:T(8,128)S(1)}, u32[]{:S(2)}, u32[]{:S(2)}) collective-permute-start(f32[8,256]{1,0:T(8,128)S(1)} %pad_maximum_fusion.m0), channel_id=1, source_target_pairs={{0,3},{1,2},{2,1},{3,0},{4,7},{5,6},{6,5},{7,4}} | collective-permute-start | bytes 24584 | tf_op jit(solution)/shard_map/ppermute | solution.py:24
  12.1 3.7 %collective-permute-start.1 = (f32[8,256]{1,0:T(8,128)S(1)}, f32[8,256]{1,0:T(8,128)S(1)}, u32[]{:S(2)}, u32[]{:S(2)}) collective-permute-start(f32[8,256]{1,0:T(8,128)S(1)} %pad_maximum_fusion.m0), channel_id=1, source_target_pairs={{0,2},{1,3},{2,0},{3,1},{4,6},{5,7},{6,4},{7,5}} | collective-permute-start | bytes 24584 | tf_op jit(solution)/shard_map/ppermute | solution.py:24
  12.5 3.7 %collective-permute-start = (f32[8,256]{1,0:T(8,128)S(1)}, f32[8,256]{1,0:T(8,128)S(1)}, u32[]{:S(2)}, u32[]{:S(2)}) collective-permute-start(f32[8,256]{1,0:T(8,128)S(1)} %pad_maximum_fusion.m0), channel_id=1, source_target_pairs={{0,1},{1,0},{2,3},{3,2},{4,5},{5,4},{6,7},{7,6}} | collective-permute-start | bytes 24584 | tf_op jit(solution)/shard_map/ppermute | solution.py:24
  13.4 2.7 copy-start.1
  13.4 55.8 %collective-permute-start.6 = (bf16[256,2304]{1,0:T(8,128)(2,1)}, bf16[256,2304]{1,0:T(8,128)(2,1)}, u32[]{:S(2)}, u32[]{:S(2)}) collective-permute-start(bf16[256,2304]{1,0:T(8,128)(2,1)} %shard_map.139.ub0.refs_2_.refs_1_), channel_id=1, source_target_pairs={{0,2},{1,3},{2,0},{3,1},{4,6},{5,7},{6,4},{7,5}} | collective-permute-start | bytes 3538952 | tf_op jit(solution)/shard_map/ppermute | solution.py:24
  15.7 0.6 copy-start.2
  15.7 53.5 %collective-permute-start.5 = (bf16[256,2304]{1,0:T(8,128)(2,1)}, bf16[256,2304]{1,0:T(8,128)(2,1)}, u32[]{:S(2)}, u32[]{:S(2)}) collective-permute-start(bf16[256,2304]{1,0:T(8,128)(2,1)} %refs_0_.5), channel_id=1, source_target_pairs={{0,2},{1,3},{2,0},{3,1},{4,6},{5,7},{6,4},{7,5}} | collective-permute-start | bytes 3538952 | tf_op jit(solution)/shard_map/ppermute | solution.py:24
  16.1 0.6 copy-start.3
  69.2 19.0 %collective-permute-start.7 = (bf16[256,2304]{1,0:T(8,128)(2,1)}, bf16[256,2304]{1,0:T(8,128)(2,1)}, u32[]{:S(2)}, u32[]{:S(2)}) collective-permute-start(bf16[256,2304]{1,0:T(8,128)(2,1)} %collective-permute-done.5.refs_1_.refs_0_), channel_id=1, source_target_pairs={{0,1},{1,0},{2,3},{3,2},{4,5},{5,4},{6,7},{7,6}} | collective-permute-start | bytes 3538952 | tf_op jit(solution)/shard_map/ppermute | solution.py:24
  85.3 4.5 %collective-permute-start.8 = (bf16[256,2304]{1,0:T(8,128)(2,1)}, bf16[256,2304]{1,0:T(8,128)(2,1)}, u32[]{:S(2)}, u32[]{:S(2)}) collective-permute-start(bf16[256,2304]{1,0:T(8,128)(2,1)} %collective-permute-done.6.refs_3_.refs_1_), channel_id=1, source_target_pairs={{0,1},{1,0},{2,3},{3,2},{4,5},{5,4},{6,7},{7,6}} | collective-permute-start | bytes 3538952 | tf_op jit(solution)/shard_map/ppermute | solution.py:24
  170.9 26.1 %collective-permute-start.9 = (bf16[512,2304]{1,0:T(8,128)(2,1)}, bf16[512,2304]{1,0:T(8,128)(2,1)}, u32[]{:S(2)}, u32[]{:S(2)}) collective-permute-start(bf16[512,2304]{1,0:T(8,128)(2,1)} %get-tuple-element.32), channel_id=1, source_target_pairs={{0,1},{1,0},{2,3},{3,2},{4,5},{5,4},{6,7},{7,6}} | collective-permute-start | bytes 7077896 | tf_op jit(solution)/shard_map/ppermute | solution.py:24
  251.4 61.5 %collective-permute-start.10 = (bf16[512,2304]{1,0:T(8,128)(2,1)}, bf16[512,2304]{1,0:T(8,128)(2,1)}, u32[]{:S(2)}, u32[]{:S(2)}) collective-permute-start(bf16[512,2304]{1,0:T(8,128)(2,1)} %get-tuple-element.37), channel_id=1, source_target_pairs={{0,1},{1,0},{2,3},{3,2},{4,5},{5,4},{6,7},{7,6}} | collective-permute-start | bytes 7077896 | tf_op jit(solution)/shard_map/ppermute | solution.py:24
  259.4 29.2 %collective-permute-start.11 = (bf16[256,2304]{1,0:T(8,128)(2,1)}, bf16[256,2304]{1,0:T(8,128)(2,1)}, u32[]{:S(2)}, u32[]{:S(2)}) collective-permute-start(bf16[256,2304]{1,0:T(8,128)(2,1)} %get-tuple-element.33), channel_id=1, source_target_pairs={{0,2},{1,3},{2,0},{3,1},{4,6},{5,7},{6,4},{7,5}} | collective-permute-start | bytes 3538952 | tf_op jit(solution)/shard_map/ppermute | solution.py:24
  259.4 53.5 %collective-permute-start.12 = (bf16[256,2304]{1,0:T(8,128)(2,1)}, bf16[256,2304]{1,0:T(8,128)(2,1)}, u32[]{:S(2)}, u32[]{:S(2)}) collective-permute-start(bf16[256,2304]{1,0:T(8,128)(2,1)} %get-tuple-element.34), channel_id=1, source_target_pairs={{0,2},{1,3},{2,0},{3,1},{4,6},{5,7},{6,4},{7,5}} | collective-permute-start | bytes 3538952 | tf_op jit(solution)/shard_map/ppermute | solution.py:24

commit v4 on v3

--- a/solution.py
+++ b/solution.py
@@ -125,7 +125,7 @@
         lo = rows
 
 
-def up_step(loc, i, n, nc, cnt, pos, us, wg, wu, x, w, sem, h, whole):
+def up_step(loc, i, n, nc, cnt, pos, us, wg, wu, x, w, sem, u, sem_u, h, whole):
     ns = w.shape[0]
 
     def copies(j):
@@ -136,9 +136,14 @@
 
     @pl.when(i == 0)
     def _():
+        tokens = [pltpu.make_async_copy(us[k], u.at[k], sem_u.at[k]) for k in range(4)]
+        for c in tokens:
+            c.start()
         for j in range(ns - 1):
             for c in copies(j):
                 c.start()
+        for c in tokens:
+            c.wait()
 
     @pl.when(i < 2)
     def _():
@@ -146,7 +151,7 @@
         for k in range(4):
             p = pos[k // 2, pl.ds(i * N_SRC + 2 * loc + k % 2, 1), :]
             pick = (lax.broadcasted_iota(I32, (SLOTS, p.shape[1]), 0).astype(F32) == p).astype(BF16)
-            rows = jnp.dot(pick, us[k][...], preferred_element_type=F32)
+            rows = jnp.dot(pick, u[k], preferred_element_type=F32)
             x[i, pl.ds(pl.multiple_of(offset(cnt, i, loc, k), 16), SLOTS), :] = rows.astype(BF16)
 
     @pl.when(i + ns - 1 < n)
@@ -177,8 +182,8 @@
         for_rows(UP_ROWS, offset(cnt, l, loc, 4), body)
 
 
-def up_kernel(loc, nc, cnt, pos, ua0, ua1, ub0, ub1, wg, wu, h, x, w, sem):
-    up_step(loc, pl.program_id(0), 2 * nc, nc, cnt, pos, (ua0, ua1, ub0, ub1), wg, wu, x, w, sem, h, False)
+def up_kernel(loc, nc, cnt, pos, ua0, ua1, ub0, ub1, wg, wu, h, x, w, sem, u, sem_u):
+    up_step(loc, pl.program_id(0), 2 * nc, nc, cnt, pos, (ua0, ua1, ub0, ub1), wg, wu, x, w, sem, u, sem_u, h, False)
 
 
 def up(loc, cnt, pos, us, wg, wu):
@@ -190,10 +195,11 @@
         functools.partial(up_kernel, loc, ff // FC),
         out_shape=jax.ShapeDtypeStruct((2, HALF, ff), BF16),
         grid_spec=pltpu.PrefetchScalarGridSpec(
-            num_scalar_prefetch=1, grid=(2 * (ff // FC),), in_specs=[vmem] * 5 + [hbm, hbm],
+            num_scalar_prefetch=1, grid=(2 * (ff // FC),), in_specs=[vmem] + [hbm] * 6,
             out_specs=pl.BlockSpec((1, HALF, FC), lambda i, c: (lax.div(i, ff // FC), 0, lax.rem(i, ff // FC))),
             scratch_shapes=[pltpu.VMEM((2, HALF, d), BF16), pltpu.VMEM((ns, d, 2 * FC), BF16),
-                            pltpu.SemaphoreType.DMA((ns, 2))]),
+                            pltpu.SemaphoreType.DMA((ns, 2)), pltpu.VMEM((4,) + us[0].shape, BF16),
+                            pltpu.SemaphoreType.DMA((4,))]),
         compiler_params=pltpu.CompilerParams(vmem_limit_bytes=63 * MIB),
         cost_estimate=pl.CostEstimate(flops=flops, bytes_accessed=flops // 512, transcendentals=0),
     )(cnt, pos, *us, wg, wu)
@@ -208,7 +214,7 @@
     wd, keep, send = next(it), next(it), next(it)
     dense_out = None if n1 else next(it)
     h, y, w2, pick, coef, s2 = [next(it) for _ in range(6)]
-    x, w1, s1 = [next(it) for _ in range(3)] if n1 else (None,) * 3
+    x, w1, s1, uv, su = [next(it) for _ in range(5)] if n1 else (None,) * 5
     w0, s0, sh = (None, None, None) if n1 else [next(it) for _ in range(3)]
     i = pl.program_id(0)
     n_tok = tab.shape[1]
@@ -272,7 +278,7 @@
                     coef[6 * mb + 3 * par + k] = jnp.broadcast_to(t[:, c:c + 1], (n_tok, 128))
 
     if n1:
-        up_step(loc, i, n1, nc, cnt, pos, us, wg, wu, x, w1, s1, h, True)
+        up_step(loc, i, n1, nc, cnt, pos, us, wg, wu, x, w1, s1, uv, su, h, True)
 
         @pl.when(i == n1 - 2)
         def _():
@@ -307,7 +313,7 @@
                         vals.append(jnp.dot(pick[4 * mb + 2 * e + par], y[e, pl.ds(r0, SLOTS), :],
                                             preferred_element_type=F32))
                     a, c0, c1 = [coef[6 * mb + 3 * par + k] for k in range(3)]
-                    u = us[par], us[2 + par]
+                    u = [uv.at[q] if n1 else us[q] for q in (par, 2 + par)]
                     for c in lanes(DC):
                         if n1:
                             cols = pl.ds(pl.multiple_of(lax.div(j, 2) * DC + c.start, 128), 128)
@@ -335,8 +341,9 @@
                pltpu.VMEM((8, n_tok, SLOTS), BF16), pltpu.VMEM((12, n_tok, 128), F32), pltpu.SemaphoreType.DMA((2,))]
     if n1:
         args = [tab, pos, *us, wg, wu, wd]
-        specs = [once(tab), once(pos)] + [once(u) for u in us] + [hbm] * 3
-        scratch += [pltpu.VMEM((2, HALF, d), BF16), pltpu.VMEM((ns1, d, 2 * FC), BF16), pltpu.SemaphoreType.DMA((ns1, 2))]
+        specs = [once(tab), once(pos)] + [hbm] * 7
+        scratch += [pltpu.VMEM((2, HALF, d), BF16), pltpu.VMEM((ns1, d, 2 * FC), BF16), pltpu.SemaphoreType.DMA((ns1, 2)),
+                    pltpu.VMEM((4,) + us[0].shape, BF16), pltpu.SemaphoreType.DMA((4,))]
     else:
         args = [tab, *us, h_in, xd, wq, wd]
         specs = [once(tab)] + [pl.BlockSpec((n_tok, DC), col)] * 4 + [hbm, once(xd), hbm, hbm]
@@ -449,10 +456,11 @@
 def solution(mesh):
     def layer(x_a, route_a, gate_a, h_b, attn_b, route_b, gate_b, w_qkv, w_o, w_gate, w_up, w_down):
         me = lax.axis_index('ep').astype(I32).reshape(1)
+        mid_b = dense(attn_b, w_o, [h_b])
         meta = jnp.concatenate([route_a.T.astype(F32), route_b.T.astype(F32), gate_a.T, gate_b.T], axis=0)
+        meta, x_a = after((meta, x_a), mid_b)
         metas = [meta] + [swap(meta, k) for k in (1, 2, 3)]
         x_par, x_cnt = swap(x_a, 1), swap(x_a, 2)
-        mid_b = dense(attn_b, w_o, [h_b])
         b_par, b_cnt = swap(mid_b, 1), swap(mid_b, 2)
         pos, tab, cnt = route(me, metas)
 

time: 321 us -> 323 us (level)
  transfers between devices with their start and end apart: 13 -> 13, of which waited for: 6 -> 6; matrix products, arithmetic and copies ran while one was open for 0% -> 0% of each run, Pallas kernels for 17% -> 18%
where the time goes in v4:
time: 323 us; the launch traced here: 322 us
  Pallas kernels  207 us (64%)
  waiting for transfers between devices  58.7 us (18%)
  starting transfers between devices  54.1 us (17%)
    pallas_call x2, Pallas kernels, ffn(): pl.pallas_call(functools.partial(ffn_kernel, loc, n0, n1, nc), out_shape=...  129 us
    ppermute x13, waiting for transfers between devices, swap(): return lax.ppermute(x, 'ep', [(i, i ^ k) for i in range(N_SRC)])  58.7 us
    ppermute x13, starting transfers between devices, swap(): return lax.ppermute(x, 'ep', [(i, i ^ k) for i in range(N_SRC)])  54.1 us
    pallas_call x1, Pallas kernels, up(): pl.pallas_call(functools.partial(up_kernel, loc, ff // FC), out_shape=jax...  52.1 us
    pallas_call x2, Pallas kernels, mix(): pl.pallas_call(functools.partial(mix_kernel, fn, len(srcs), bw), out_shap...  13.2 us
    pallas_call x1, Pallas kernels, dense(): pl.pallas_call(dense_kernel, out_shape=jax.ShapeDtypeStruct((n, width), B...  7.82 us
  transfers between devices with their start and end apart: 13, of which 6 were waited for; matrix products, arithmetic and copies ran while one was open for 0% of the time, Pallas kernels for 18%

profile of v4, /device:TPU:0, one launch (start us, length us, event | category | flops | bytes accessed | tf_op | source)
XLA Modules:
  0.0 322.1 jit_solution(2450779206658807273)
XLA Ops:
  0.6 0.7 convert_bitcast_fusion
  1.3 7.8 %shard_map.139.ub0.refs_2_.refs_1_ = bf16[256,2304]{1,0:T(8,128)(2,1)} custom-call(bf16[256,2304]{1,0:T(8,128)(2,1)} %x.1, bf16[2304,2304]{1,0:T(8,128)(2,1)} %w.1, bf16[256,2304]{1,0:T(8,128)(2,1)} %refs_5_.3), custom_call_target="tpu_custom_call" | custom-call | flops 2717908992 | bytes 10616832 | tf_op jit(solution)/shard_map/pallas_call | solution.py:447
  9.2 0.0 copy-start
  9.2 0.9 collective-permute-start.3
  10.1 0.0 collective-permute-start.4
  10.1 2.6 collective-permute-start.2
  12.7 0.4 collective-permute-start.1
  13.0 0.1 collective-permute-start
  13.2 0.9 collective-permute-done.2.m3
  14.1 2.1 collective-permute-start.5
  16.1 0.2 collective-permute-done.1.m2
  16.3 0.4 collective-permute-start.6
  16.7 0.2 copy-done.2
  16.9 0.4 copy-done.3
  17.3 1.8 route.1
  19.1 0.0 collective-permute-done.3.ua1.refs_1_
  19.1 52.1 %shard_map.140.refs_4_ = bf16[2,512,5760]{2,1,0:T(8,128)(2,1)} custom-call(s32[2,8,128]{2,1,0:T(8,128)} %get-tuple-element.39.cnt, f32[2,8,256]{2,1,0:T(8,128)} %get-tuple-element.27.pos.refs_0_, bf16[256,2304]{1,0:T(8,128)(2,1)} %refs_0_.3, bf16[256,2304]{1,0:T(8,128)(2,1)} %collective-permute-done.3.ua1.refs_1_, ...), custom_call_target="tpu_custom_call" | custom-call | flops 54358179840 | bytes 106168320 | tf_op jit(solution)/shard_map/pallas_call | solution.py:194
  71.2 0.0 collective-permute-done.5.refs_1_.refs_0_
  71.2 16.2 %collective-permute-start.7 = (bf16[256,2304]{1,0:T(8,128)(2,1)}, bf16[256,2304]{1,0:T(8,128)(2,1)}, u32[]{:S(2)}, u32[]{:S(2)}) collective-permute-start(bf16[256,2304]{1,0:T(8,128)(2,1)} %collective-permute-done.5.refs_1_.refs_0_), channel_id=1, source_target_pairs={{0,1},{1,0},{2,3},{3,2},{4,5},{5,4},{6,7},{7,6}} | collective-permute-start | bytes 3538952 | tf_op jit(solution)/shard_map/ppermute | solution.py:24
  87.4 0.0 collective-permute-start.8
  87.4 2.9 spread.1
  90.3 1.6 collective-permute-done.8.refs_4_
  91.9 80.9 %shard_map.141 = (bf16[512,2304]{1,0:T(8,128)(2,1)}, bf16[512,2304]{1,0:T(8,128)(2,1)}) custom-call(s32[2,8,128]{2,1,0:T(8,128)} %get-tuple-element.39.cnt, f32[2,256,128]{2,1,0:T(8,128)} %get-tuple-element.29.tab, f32[2,8,256]{2,1,0:T(8,128)} %get-tuple-element.27.pos.refs_0_, bf16[256,2304]{1,0:T(8,128)(2,1)} %collective-permute-done.5.refs_1_.refs_0_, ...), custom_call_target="tpu_custom_call" | custom-call | flops 81537269760 | bytes 159252480 | tf_op jit(solution)/shard_map/pallas_call | solution.py:357
  172.8 21.5 %collective-permute-start.9 = (bf16[512,2304]{1,0:T(8,128)(2,1)}, bf16[512,2304]{1,0:T(8,128)(2,1)}, u32[]{:S(2)}, u32[]{:S(2)}) collective-permute-start(bf16[512,2304]{1,0:T(8,128)(2,1)} %get-tuple-element.36), channel_id=1, source_target_pairs={{0,1},{1,0},{2,3},{3,2},{4,5},{5,4},{6,7},{7,6}} | collective-permute-start | bytes 7077896 | tf_op jit(solution)/shard_map/ppermute | solution.py:24
  194.3 4.5 %collective-permute-done.9.refs_3_ = bf16[512,2304]{1,0:T(8,128)(2,1)} collective-permute-done((bf16[512,2304]{1,0:T(8,128)(2,1)}, bf16[512,2304]{1,0:T(8,128)(2,1)}, u32[]{:S(2)}, u32[]{:S(2)}) %collective-permute-start.9) | collective-permute-done | bytes 2359328 | tf_op jit(solution)/shard_map/ppermute | solution.py:24
  198.8 5.9 %shard_map.142 = (bf16[256,2304]{1,0:T(8,128)(2,1)}, bf16[256,2304]{1,0:T(8,128)(2,1)}) custom-call(f32[6,256,128]{2,1,0:T(8,128)} %get-tuple-element.31.coef, bf16[256,2304]{1,0:T(8,128)(2,1)} %collective-permute-done.5.refs_1_.refs_0_, bf16[256,2304]{1,0:T(8,128)(2,1)} %collective-permute-done.6.refs_3_.refs_1_, ...), custom_call_target="tpu_custom_call" | custom-call | flops 1000000000 | bytes 1000000 | tf_op jit(solution)/shard_map/pallas_call | solution.py:426
  204.7 48.5 %shard_map.143 = (bf16[512,2304]{1,0:T(8,128)(2,1)}, bf16[512,2304]{1,0:T(8,128)(2,1)}, bf16[256,6912]{1,0:T(8,128)(2,1)}) custom-call(s32[2,8,128]{2,1,0:T(8,128)} %get-tuple-element.39.cnt, f32[2,256,128]{2,1,0:T(8,128)} %get-tuple-element.29.tab, bf16[256,2304]{1,0:T(8,128)(2,1)} %refs_0_.3, bf16[256,2304]{1,0:T(8,128)(2,1)} %collective-permute-done.3.ua1.refs_1_, ...), custom_call_target="tpu_custom_call" | custom-call | flops 40768634880 | bytes 79626240 | tf_op jit(solution)/shard_map/pallas_call | solution.py:357
  253.2 8.0 %collective-permute-start.10 = (bf16[512,2304]{1,0:T(8,128)(2,1)}, bf16[512,2304]{1,0:T(8,128)(2,1)}, u32[]{:S(2)}, u32[]{:S(2)}) collective-permute-start(bf16[512,2304]{1,0:T(8,128)(2,1)} %get-tuple-element.41), channel_id=1, source_target_pairs={{0,1},{1,0},{2,3},{3,2},{4,5},{5,4},{6,7},{7,6}} | collective-permute-start | bytes 7077896 | tf_op jit(solution)/shard_map/ppermute | solution.py:24
  261.2 2.0 collective-permute-start.12
  263.2 27.1 %collective-permute-done.11.refs_4_ = bf16[256,2304]{1,0:T(8,128)(2,1)} collective-permute-done((bf16[256,2304]{1,0:T(8,128)(2,1)}, bf16[256,2304]{1,0:T(8,128)(2,1)}, u32[]{:S(2)}, u32[]{:S(2)}) %collective-permute-start.11) | collective-permute-done | bytes 1179680 | tf_op jit(solution)/shard_map/ppermute | solution.py:24
  290.3 24.3 %collective-permute-done.12.refs_5_ = bf16[256,2304]{1,0:T(8,128)(2,1)} collective-permute-done((bf16[256,2304]{1,0:T(8,128)(2,1)}, bf16[256,2304]{1,0:T(8,128)(2,1)}, u32[]{:S(2)}, u32[]{:S(2)}) %collective-permute-start.12) | collective-permute-done | bytes 1179680 | tf_op jit(solution)/shard_map/ppermute | solution.py:24
  314.7 7.3 %shard_map.144 = (bf16[256,2304]{1,0:T(8,128)(2,1)}, bf16[256,2304]{1,0:T(8,128)(2,1)}) custom-call(f32[12,256,128]{2,1,0:T(8,128)} %get-tuple-element.30.coef, bf16[256,2304]{1,0:T(8,128)(2,1)} %refs_0_.3, bf16[256,2304]{1,0:T(8,128)(2,1)} %shard_map.139.ub0.refs_2_.refs_1_, bf16[512,2304]{1,0:T(8,128)(2,1)} %get-tuple-element.40.refs_2_, ...), custom_call_target="tpu_custom_call" | custom-call | flops 1000000000 | bytes 1000000 | tf_op jit(solution)/shard_map/pallas_call | solution.py:426
  (16 shorter events, 0.0 us)
Async XLA Ops:
  1.3 7.8 %copy-start.4 = (f32[256,2]{0,1:T(2,128)S(1)}, f32[256,2]{0,1:T(2,128)}, u32[]{:S(2)}) copy-start(f32[256,2]{0,1:T(2,128)} %param.18) | copy-start | bytes 6148
  1.3 7.8 %copy-start.5 = (f32[256,2]{0,1:T(2,128)S(1)}, f32[256,2]{0,1:T(2,128)}, u32[]{:S(2)}) copy-start(f32[256,2]{0,1:T(2,128)} %param.14) | copy-start | bytes 6148
  9.2 7.5 %copy-start = (f32[8,256]{1,0:T(8,128)}, f32[8,256]{1,0:T(8,128)S(1)}, u32[]{:S(2)}) copy-start(f32[8,256]{1,0:T(8,128)S(1)} %pad_maximum_fusion.m0) | copy-start | bytes 24580
  9.2 9.9 %collective-permute-start.3 = (bf16[256,2304]{1,0:T(8,128)(2,1)}, bf16[256,2304]{1,0:T(8,128)(2,1)}, u32[]{:S(2)}, u32[]{:S(2)}) collective-permute-start(bf16[256,2304]{1,0:T(8,128)(2,1)} %refs_0_.3), channel_id=1, source_target_pairs={{0,1},{1,0},{2,3},{3,2},{4,5},{5,4},{6,7},{7,6}} | collective-permute-start | bytes 3538952 | tf_op jit(solution)/shard_map/ppermute | solution.py:24
  10.1 9.0 %collective-permute-start.4 = (bf16[256,2304]{1,0:T(8,128)(2,1)}, bf16[256,2304]{1,0:T(8,128)(2,1)}, u32[]{:S(2)}, u32[]{:S(2)}) collective-permute-start(bf16[256,2304]{1,0:T(8,128)(2,1)} %shard_map.139.ub0.refs_2_.refs_1_), channel_id=1, source_target_pairs={{0,1},{1,0},{2,3},{3,2},{4,5},{5,4},{6,7},{7,6}} | collective-permute-start | bytes 3538952 | tf_op jit(solution)/shard_map/ppermute | solution.py:24
  10.1 4.0 %collective-permute-start.2 = (f32[8,256]{1,0:T(8,128)S(1)}, f32[8,256]{1,0:T(8,128)S(1)}, u32[]{:S(2)}, u32[]{:S(2)}) collective-permute-start(f32[8,256]{1,0:T(8,128)S(1)} %pad_maximum_fusion.m0), channel_id=1, source_target_pairs={{0,3},{1,2},{2,1},{3,0},{4,7},{5,6},{6,5},{7,4}} | collective-permute-start | bytes 24584 | tf_op jit(solution)/shard_map/ppermute | solution.py:24
  12.7 3.7 %collective-permute-start.1 = (f32[8,256]{1,0:T(8,128)S(1)}, f32[8,256]{1,0:T(8,128)S(1)}, u32[]{:S(2)}, u32[]{:S(2)}) collective-permute-start(f32[8,256]{1,0:T(8,128)S(1)} %pad_maximum_fusion.m0), channel_id=1, source_target_pairs={{0,2},{1,3},{2,0},{3,1},{4,6},{5,7},{6,4},{7,5}} | collective-permute-start | bytes 24584 | tf_op jit(solution)/shard_map/ppermute | solution.py:24
  13.0 3.7 %collective-permute-start = (f32[8,256]{1,0:T(8,128)S(1)}, f32[8,256]{1,0:T(8,128)S(1)}, u32[]{:S(2)}, u32[]{:S(2)}) collective-permute-start(f32[8,256]{1,0:T(8,128)S(1)} %pad_maximum_fusion.m0), channel_id=1, source_target_pairs={{0,1},{1,0},{2,3},{3,2},{4,5},{5,4},{6,7},{7,6}} | collective-permute-start | bytes 24584 | tf_op jit(solution)/shard_map/ppermute | solution.py:24
  14.1 2.7 copy-start.1
  14.1 57.2 %collective-permute-start.5 = (bf16[256,2304]{1,0:T(8,128)(2,1)}, bf16[256,2304]{1,0:T(8,128)(2,1)}, u32[]{:S(2)}, u32[]{:S(2)}) collective-permute-start(bf16[256,2304]{1,0:T(8,128)(2,1)} %refs_0_.3), channel_id=1, source_target_pairs={{0,2},{1,3},{2,0},{3,1},{4,6},{5,7},{6,4},{7,5}} | collective-permute-start | bytes 3538952 | tf_op jit(solution)/shard_map/ppermute | solution.py:24
  16.3 0.6 copy-start.2
  16.3 54.9 %collective-permute-start.6 = (bf16[256,2304]{1,0:T(8,128)(2,1)}, bf16[256,2304]{1,0:T(8,128)(2,1)}, u32[]{:S(2)}, u32[]{:S(2)}) collective-permute-start(bf16[256,2304]{1,0:T(8,128)(2,1)} %shard_map.139.ub0.refs_2_.refs_1_), channel_id=1, source_target_pairs={{0,2},{1,3},{2,0},{3,1},{4,6},{5,7},{6,4},{7,5}} | collective-permute-start | bytes 3538952 | tf_op jit(solution)/shard_map/ppermute | solution.py:24
  16.7 0.6 copy-start.3
  71.2 19.1 %collective-permute-start.7 = (bf16[256,2304]{1,0:T(8,128)(2,1)}, bf16[256,2304]{1,0:T(8,128)(2,1)}, u32[]{:S(2)}, u32[]{:S(2)}) collective-permute-start(bf16[256,2304]{1,0:T(8,128)(2,1)} %collective-permute-done.5.refs_1_.refs_0_), channel_id=1, source_target_pairs={{0,1},{1,0},{2,3},{3,2},{4,5},{5,4},{6,7},{7,6}} | collective-permute-start | bytes 3538952 | tf_op jit(solution)/shard_map/ppermute | solution.py:24
  87.4 4.5 %collective-permute-start.8 = (bf16[256,2304]{1,0:T(8,128)(2,1)}, bf16[256,2304]{1,0:T(8,128)(2,1)}, u32[]{:S(2)}, u32[]{:S(2)}) collective-permute-start(bf16[256,2304]{1,0:T(8,128)(2,1)} %collective-permute-done.6.refs_3_.refs_1_), channel_id=1, source_target_pairs={{0,1},{1,0},{2,3},{3,2},{4,5},{5,4},{6,7},{7,6}} | collective-permute-start | bytes 3538952 | tf_op jit(solution)/shard_map/ppermute | solution.py:24
  172.8 26.0 %collective-permute-start.9 = (bf16[512,2304]{1,0:T(8,128)(2,1)}, bf16[512,2304]{1,0:T(8,128)(2,1)}, u32[]{:S(2)}, u32[]{:S(2)}) collective-permute-start(bf16[512,2304]{1,0:T(8,128)(2,1)} %get-tuple-element.36), channel_id=1, source_target_pairs={{0,1},{1,0},{2,3},{3,2},{4,5},{5,4},{6,7},{7,6}} | collective-permute-start | bytes 7077896 | tf_op jit(solution)/shard_map/ppermute | solution.py:24
  253.2 61.5 %collective-permute-start.10 = (bf16[512,2304]{1,0:T(8,128)(2,1)}, bf16[512,2304]{1,0:T(8,128)(2,1)}, u32[]{:S(2)}, u32[]{:S(2)}) collective-permute-start(bf16[512,2304]{1,0:T(8,128)(2,1)} %get-tuple-element.41), channel_id=1, source_target_pairs={{0,1},{1,0},{2,3},{3,2},{4,5},{5,4},{6,7},{7,6}} | collective-permute-start | bytes 7077896 | tf_op jit(solution)/shard_map/ppermute | solution.py:24
  261.2 29.2 %collective-permute-start.11 = (bf16[256,2304]{1,0:T(8,128)(2,1)}, bf16[256,2304]{1,0:T(8,128)(2,1)}, u32[]{:S(2)}, u32[]{:S(2)}) collective-permute-start(bf16[256,2304]{1,0:T(8,128)(2,1)} %get-tuple-element.37), channel_id=1, source_target_pairs={{0,2},{1,3},{2,0},{3,1},{4,6},{5,7},{6,4},{7,5}} | collective-permute-start | bytes 3538952 | tf_op jit(solution)/shard_map/ppermute | solution.py:24
  261.2 53.5 %collective-permute-start.12 = (bf16[256,2304]{1,0:T(8,128)(2,1)}, bf16[256,2304]{1,0:T(8,128)(2,1)}, u32[]{:S(2)}, u32[]{:S(2)}) collective-permute-start(bf16[256,2304]{1,0:T(8,128)(2,1)} %get-tuple-element.38), channel_id=1, source_target_pairs={{0,2},{1,3},{2,0},{3,1},{4,6},{5,7},{6,4},{7,5}} | collective-permute-start | bytes 3538952 | tf_op jit(solution)/shard_map/ppermute | solution.py:24

commit v5 on v4

--- a/solution.py
+++ b/solution.py
@@ -136,7 +136,7 @@
 
     @pl.when(i == 0)
     def _():
-        tokens = [pltpu.make_async_copy(us[k], u.at[k], sem_u.at[k]) for k in range(4)]
+        tokens = [] if u is None else [pltpu.make_async_copy(us[k], u.at[k], sem_u.at[k]) for k in range(4)]
         for c in tokens:
             c.start()
         for j in range(ns - 1):
@@ -151,7 +151,7 @@
         for k in range(4):
             p = pos[k // 2, pl.ds(i * N_SRC + 2 * loc + k % 2, 1), :]
             pick = (lax.broadcasted_iota(I32, (SLOTS, p.shape[1]), 0).astype(F32) == p).astype(BF16)
-            rows = jnp.dot(pick, u[k], preferred_element_type=F32)
+            rows = jnp.dot(pick, us[k][...] if u is None else u[k], preferred_element_type=F32)
             x[i, pl.ds(pl.multiple_of(offset(cnt, i, loc, k), 16), SLOTS), :] = rows.astype(BF16)
 
     @pl.when(i + ns - 1 < n)
@@ -182,8 +182,8 @@
         for_rows(UP_ROWS, offset(cnt, l, loc, 4), body)
 
 
-def up_kernel(loc, nc, cnt, pos, ua0, ua1, ub0, ub1, wg, wu, h, x, w, sem, u, sem_u):
-    up_step(loc, pl.program_id(0), 2 * nc, nc, cnt, pos, (ua0, ua1, ub0, ub1), wg, wu, x, w, sem, u, sem_u, h, False)
+def up_kernel(loc, nc, cnt, pos, ua0, ua1, ub0, ub1, wg, wu, h, x, w, sem):
+    up_step(loc, pl.program_id(0), 2 * nc, nc, cnt, pos, (ua0, ua1, ub0, ub1), wg, wu, x, w, sem, None, None, h, False)
 
 
 def up(loc, cnt, pos, us, wg, wu):
@@ -195,11 +195,10 @@
         functools.partial(up_kernel, loc, ff // FC),
         out_shape=jax.ShapeDtypeStruct((2, HALF, ff), BF16),
         grid_spec=pltpu.PrefetchScalarGridSpec(
-            num_scalar_prefetch=1, grid=(2 * (ff // FC),), in_specs=[vmem] + [hbm] * 6,
+            num_scalar_prefetch=1, grid=(2 * (ff // FC),), in_specs=[vmem] * 5 + [hbm] * 2,
             out_specs=pl.BlockSpec((1, HALF, FC), lambda i, c: (lax.div(i, ff // FC), 0, lax.rem(i, ff // FC))),
             scratch_shapes=[pltpu.VMEM((2, HALF, d), BF16), pltpu.VMEM((ns, d, 2 * FC), BF16),
-                            pltpu.SemaphoreType.DMA((ns, 2)), pltpu.VMEM((4,) + us[0].shape, BF16),
-                            pltpu.SemaphoreType.DMA((4,))]),
+                            pltpu.SemaphoreType.DMA((ns, 2))]),
         compiler_params=pltpu.CompilerParams(vmem_limit_bytes=63 * MIB),
         cost_estimate=pl.CostEstimate(flops=flops, bytes_accessed=flops // 512, transcendentals=0),
     )(cnt, pos, *us, wg, wu)

time: 323 us -> 321 us (level)
  transfers between devices with their start and end apart: 13 -> 13, of which waited for: 6 -> 6; matrix products, arithmetic and copies ran while one was open for 0% -> 0% of each run, Pallas kernels for 18% -> 17%
where the time goes in v5:
time: 321 us
  Pallas kernels  206 us (64%)
  waiting for transfers between devices  58.7 us (18%)
  starting transfers between devices  54 us (17%)
    pallas_call x2, Pallas kernels, ffn(): pl.pallas_call(functools.partial(ffn_kernel, loc, n0, n1, nc), out_shape=...  129 us
    ppermute x13, waiting for transfers between devices, swap(): return lax.ppermute(x, 'ep', [(i, i ^ k) for i in range(N_SRC)])  58.7 us
    ppermute x13, starting transfers between devices, swap(): return lax.ppermute(x, 'ep', [(i, i ^ k) for i in range(N_SRC)])  54 us
    pallas_call x1, Pallas kernels, up(): pl.pallas_call(functools.partial(up_kernel, loc, ff // FC), out_shape=jax...  50.6 us
    pallas_call x2, Pallas kernels, mix(): pl.pallas_call(functools.partial(mix_kernel, fn, len(srcs), bw), out_shap...  13.2 us
    pallas_call x1, Pallas kernels, dense(): pl.pallas_call(dense_kernel, out_shape=jax.ShapeDtypeStruct((n, width), B...  7.82 us
  transfers between devices with their start and end apart: 13, of which 6 were waited for; matrix products, arithmetic and copies ran while one was open for 0% of the time, Pallas kernels for 17%

profile of v5, /device:TPU:0, one launch (start us, length us, event | category | flops | bytes accessed | tf_op | source)
XLA Modules:
  0.0 320.6 jit_solution(3070345750701829147)
XLA Ops:
  0.6 0.7 convert_bitcast_fusion
  1.3 7.8 %shard_map.139.ub0.refs_2_.refs_1_ = bf16[256,2304]{1,0:T(8,128)(2,1)} custom-call(bf16[256,2304]{1,0:T(8,128)(2,1)} %x.1, bf16[2304,2304]{1,0:T(8,128)(2,1)} %w.1, bf16[256,2304]{1,0:T(8,128)(2,1)} %refs_5_.3), custom_call_target="tpu_custom_call" | custom-call | flops 2717908992 | bytes 10616832 | tf_op jit(solution)/shard_map/pallas_call | solution.py:446
  9.2 0.0 copy-start
  9.2 0.9 collective-permute-start.3
  10.1 0.0 collective-permute-start.4
  10.1 2.6 collective-permute-start.2
  12.7 0.4 collective-permute-start.1
  13.0 0.1 collective-permute-start
  13.2 0.9 collective-permute-done.2.m3
  14.1 2.1 collective-permute-start.5
  16.1 0.2 collective-permute-done.1.m2
  16.3 0.4 collective-permute-start.6
  16.7 0.2 copy-done.2
  16.9 0.4 copy-done.3
  17.3 1.8 route.1
  19.1 0.0 collective-permute-done.3.ua1.refs_1_
  19.1 50.6 %shard_map.140.refs_4_ = bf16[2,512,5760]{2,1,0:T(8,128)(2,1)} custom-call(s32[2,8,128]{2,1,0:T(8,128)} %get-tuple-element.39.cnt, f32[2,8,256]{2,1,0:T(8,128)} %get-tuple-element.27.pos.refs_0_, bf16[256,2304]{1,0:T(8,128)(2,1)} %refs_0_.3, bf16[256,2304]{1,0:T(8,128)(2,1)} %collective-permute-done.3.ua1.refs_1_, ...), custom_call_target="tpu_custom_call" | custom-call | flops 54358179840 | bytes 106168320 | tf_op jit(solution)/shard_map/pallas_call | solution.py:194
  69.7 0.0 collective-permute-done.5.refs_1_.refs_0_
  69.7 16.1 %collective-permute-start.7 = (bf16[256,2304]{1,0:T(8,128)(2,1)}, bf16[256,2304]{1,0:T(8,128)(2,1)}, u32[]{:S(2)}, u32[]{:S(2)}) collective-permute-start(bf16[256,2304]{1,0:T(8,128)(2,1)} %collective-permute-done.5.refs_1_.refs_0_), channel_id=1, source_target_pairs={{0,1},{1,0},{2,3},{3,2},{4,5},{5,4},{6,7},{7,6}} | collective-permute-start | bytes 3538952 | tf_op jit(solution)/shard_map/ppermute | solution.py:24
  85.9 0.0 collective-permute-start.8
  85.9 2.9 spread.1
  88.8 1.6 collective-permute-done.8.refs_4_
  90.4 80.9 %shard_map.141 = (bf16[512,2304]{1,0:T(8,128)(2,1)}, bf16[512,2304]{1,0:T(8,128)(2,1)}) custom-call(s32[2,8,128]{2,1,0:T(8,128)} %get-tuple-element.39.cnt, f32[2,256,128]{2,1,0:T(8,128)} %get-tuple-element.29.tab, f32[2,8,256]{2,1,0:T(8,128)} %get-tuple-element.27.pos.refs_0_, bf16[256,2304]{1,0:T(8,128)(2,1)} %collective-permute-done.5.refs_1_.refs_0_, ...), custom_call_target="tpu_custom_call" | custom-call | flops 81537269760 | bytes 159252480 | tf_op jit(solution)/shard_map/pallas_call | solution.py:356
  171.3 21.5 %collective-permute-start.9 = (bf16[512,2304]{1,0:T(8,128)(2,1)}, bf16[512,2304]{1,0:T(8,128)(2,1)}, u32[]{:S(2)}, u32[]{:S(2)}) collective-permute-start(bf16[512,2304]{1,0:T(8,128)(2,1)} %get-tuple-element.36), channel_id=1, source_target_pairs={{0,1},{1,0},{2,3},{3,2},{4,5},{5,4},{6,7},{7,6}} | collective-permute-start | bytes 7077896 | tf_op jit(solution)/shard_map/ppermute | solution.py:24
  192.7 4.5 %collective-permute-done.9.refs_3_ = bf16[512,2304]{1,0:T(8,128)(2,1)} collective-permute-done((bf16[512,2304]{1,0:T(8,128)(2,1)}, bf16[512,2304]{1,0:T(8,128)(2,1)}, u32[]{:S(2)}, u32[]{:S(2)}) %collective-permute-start.9) | collective-permute-done | bytes 2359328 | tf_op jit(solution)/shard_map/ppermute | solution.py:24
  197.2 5.9 %shard_map.142 = (bf16[256,2304]{1,0:T(8,128)(2,1)}, bf16[256,2304]{1,0:T(8,128)(2,1)}) custom-call(f32[6,256,128]{2,1,0:T(8,128)} %get-tuple-element.31.coef, bf16[256,2304]{1,0:T(8,128)(2,1)} %collective-permute-done.5.refs_1_.refs_0_, bf16[256,2304]{1,0:T(8,128)(2,1)} %collective-permute-done.6.refs_3_.refs_1_, ...), custom_call_target="tpu_custom_call" | custom-call | flops 1000000000 | bytes 1000000 | tf_op jit(solution)/shard_map/pallas_call | solution.py:425
  203.2 48.5 %shard_map.143 = (bf16[512,2304]{1,0:T(8,128)(2,1)}, bf16[512,2304]{1,0:T(8,128)(2,1)}, bf16[256,6912]{1,0:T(8,128)(2,1)}) custom-call(s32[2,8,128]{2,1,0:T(8,128)} %get-tuple-element.39.cnt, f32[2,256,128]{2,1,0:T(8,128)} %get-tuple-element.29.tab, bf16[256,2304]{1,0:T(8,128)(2,1)} %refs_0_.3, bf16[256,2304]{1,0:T(8,128)(2,1)} %collective-permute-done.3.ua1.refs_1_, ...), custom_call_target="tpu_custom_call" | custom-call | flops 40768634880 | bytes 79626240 | tf_op jit(solution)/shard_map/pallas_call | solution.py:356
  251.7 8.0 %collective-permute-start.10 = (bf16[512,2304]{1,0:T(8,128)(2,1)}, bf16[512,2304]{1,0:T(8,128)(2,1)}, u32[]{:S(2)}, u32[]{:S(2)}) collective-permute-start(bf16[512,2304]{1,0:T(8,128)(2,1)} %get-tuple-element.41), channel_id=1, source_target_pairs={{0,1},{1,0},{2,3},{3,2},{4,5},{5,4},{6,7},{7,6}} | collective-permute-start | bytes 7077896 | tf_op jit(solution)/shard_map/ppermute | solution.py:24
  259.7 2.0 collective-permute-start.12
  261.7 27.1 %collective-permute-done.11.refs_4_ = bf16[256,2304]{1,0:T(8,128)(2,1)} collective-permute-done((bf16[256,2304]{1,0:T(8,128)(2,1)}, bf16[256,2304]{1,0:T(8,128)(2,1)}, u32[]{:S(2)}, u32[]{:S(2)}) %collective-permute-start.11) | collective-permute-done | bytes 1179680 | tf_op jit(solution)/shard_map/ppermute | solution.py:24
  288.8 24.3 %collective-permute-done.12.refs_5_ = bf16[256,2304]{1,0:T(8,128)(2,1)} collective-permute-done((bf16[256,2304]{1,0:T(8,128)(2,1)}, bf16[256,2304]{1,0:T(8,128)(2,1)}, u32[]{:S(2)}, u32[]{:S(2)}) %collective-permute-start.12) | collective-permute-done | bytes 1179680 | tf_op jit(solution)/shard_map/ppermute | solution.py:24
  313.2 7.3 %shard_map.144 = (bf16[256,2304]{1,0:T(8,128)(2,1)}, bf16[256,2304]{1,0:T(8,128)(2,1)}) custom-call(f32[12,256,128]{2,1,0:T(8,128)} %get-tuple-element.30.coef, bf16[256,2304]{1,0:T(8,128)(2,1)} %refs_0_.3, bf16[256,2304]{1,0:T(8,128)(2,1)} %shard_map.139.ub0.refs_2_.refs_1_, bf16[512,2304]{1,0:T(8,128)(2,1)} %get-tuple-element.40.refs_2_, ...), custom_call_target="tpu_custom_call" | custom-call | flops 1000000000 | bytes 1000000 | tf_op jit(solution)/shard_map/pallas_call | solution.py:425
  (16 shorter events, 0.0 us)
Async XLA Ops:
  1.3 7.8 %copy-start.4 = (f32[256,2]{0,1:T(2,128)S(1)}, f32[256,2]{0,1:T(2,128)}, u32[]{:S(2)}) copy-start(f32[256,2]{0,1:T(2,128)} %param.18) | copy-start | bytes 6148
  1.3 7.8 %copy-start.5 = (f32[256,2]{0,1:T(2,128)S(1)}, f32[256,2]{0,1:T(2,128)}, u32[]{:S(2)}) copy-start(f32[256,2]{0,1:T(2,128)} %param.14) | copy-start | bytes 6148
  9.2 7.5 %copy-start = (f32[8,256]{1,0:T(8,128)}, f32[8,256]{1,0:T(8,128)S(1)}, u32[]{:S(2)}) copy-start(f32[8,256]{1,0:T(8,128)S(1)} %pad_maximum_fusion.m0) | copy-start | bytes 24580
  9.2 9.9 %collective-permute-start.3 = (bf16[256,2304]{1,0:T(8,128)(2,1)}, bf16[256,2304]{1,0:T(8,128)(2,1)}, u32[]{:S(2)}, u32[]{:S(2)}) collective-permute-start(bf16[256,2304]{1,0:T(8,128)(2,1)} %refs_0_.3), channel_id=1, source_target_pairs={{0,1},{1,0},{2,3},{3,2},{4,5},{5,4},{6,7},{7,6}} | collective-permute-start | bytes 3538952 | tf_op jit(solution)/shard_map/ppermute | solution.py:24
  10.1 9.0 %collective-permute-start.4 = (bf16[256,2304]{1,0:T(8,128)(2,1)}, bf16[256,2304]{1,0:T(8,128)(2,1)}, u32[]{:S(2)}, u32[]{:S(2)}) collective-permute-start(bf16[256,2304]{1,0:T(8,128)(2,1)} %shard_map.139.ub0.refs_2_.refs_1_), channel_id=1, source_target_pairs={{0,1},{1,0},{2,3},{3,2},{4,5},{5,4},{6,7},{7,6}} | collective-permute-start | bytes 3538952 | tf_op jit(solution)/shard_map/ppermute | solution.py:24
  10.1 4.0 %collective-permute-start.2 = (f32[8,256]{1,0:T(8,128)S(1)}, f32[8,256]{1,0:T(8,128)S(1)}, u32[]{:S(2)}, u32[]{:S(2)}) collective-permute-start(f32[8,256]{1,0:T(8,128)S(1)} %pad_maximum_fusion.m0), channel_id=1, source_target_pairs={{0,3},{1,2},{2,1},{3,0},{4,7},{5,6},{6,5},{7,4}} | collective-permute-start | bytes 24584 | tf_op jit(solution)/shard_map/ppermute | solution.py:24
  12.7 3.7 %collective-permute-start.1 = (f32[8,256]{1,0:T(8,128)S(1)}, f32[8,256]{1,0:T(8,128)S(1)}, u32[]{:S(2)}, u32[]{:S(2)}) collective-permute-start(f32[8,256]{1,0:T(8,128)S(1)} %pad_maximum_fusion.m0), channel_id=1, source_target_pairs={{0,2},{1,3},{2,0},{3,1},{4,6},{5,7},{6,4},{7,5}} | collective-permute-start | bytes 24584 | tf_op jit(solution)/shard_map/ppermute | solution.py:24
  13.0 3.7 %collective-permute-start = (f32[8,256]{1,0:T(8,128)S(1)}, f32[8,256]{1,0:T(8,128)S(1)}, u32[]{:S(2)}, u32[]{:S(2)}) collective-permute-start(f32[8,256]{1,0:T(8,128)S(1)} %pad_maximum_fusion.m0), channel_id=1, source_target_pairs={{0,1},{1,0},{2,3},{3,2},{4,5},{5,4},{6,7},{7,6}} | collective-permute-start | bytes 24584 | tf_op jit(solution)/shard_map/ppermute | solution.py:24
  14.1 2.7 copy-start.1
  14.1 55.7 %collective-permute-start.5 = (bf16[256,2304]{1,0:T(8,128)(2,1)}, bf16[256,2304]{1,0:T(8,128)(2,1)}, u32[]{:S(2)}, u32[]{:S(2)}) collective-permute-start(bf16[256,2304]{1,0:T(8,128)(2,1)} %refs_0_.3), channel_id=1, source_target_pairs={{0,2},{1,3},{2,0},{3,1},{4,6},{5,7},{6,4},{7,5}} | collective-permute-start | bytes 3538952 | tf_op jit(solution)/shard_map/ppermute | solution.py:24
  16.3 0.6 copy-start.2
  16.3 53.4 %collective-permute-start.6 = (bf16[256,2304]{1,0:T(8,128)(2,1)}, bf16[256,2304]{1,0:T(8,128)(2,1)}, u32[]{:S(2)}, u32[]{:S(2)}) collective-permute-start(bf16[256,2304]{1,0:T(8,128)(2,1)} %shard_map.139.ub0.refs_2_.refs_1_), channel_id=1, source_target_pairs={{0,2},{1,3},{2,0},{3,1},{4,6},{5,7},{6,4},{7,5}} | collective-permute-start | bytes 3538952 | tf_op jit(solution)/shard_map/ppermute | solution.py:24
  16.7 0.6 copy-start.3
  69.7 19.0 %collective-permute-start.7 = (bf16[256,2304]{1,0:T(8,128)(2,1)}, bf16[256,2304]{1,0:T(8,128)(2,1)}, u32[]{:S(2)}, u32[]{:S(2)}) collective-permute-start(bf16[256,2304]{1,0:T(8,128)(2,1)} %collective-permute-done.5.refs_1_.refs_0_), channel_id=1, source_target_pairs={{0,1},{1,0},{2,3},{3,2},{4,5},{5,4},{6,7},{7,6}} | collective-permute-start | bytes 3538952 | tf_op jit(solution)/shard_map/ppermute | solution.py:24
  85.9 4.5 %collective-permute-start.8 = (bf16[256,2304]{1,0:T(8,128)(2,1)}, bf16[256,2304]{1,0:T(8,128)(2,1)}, u32[]{:S(2)}, u32[]{:S(2)}) collective-permute-start(bf16[256,2304]{1,0:T(8,128)(2,1)} %collective-permute-done.6.refs_3_.refs_1_), channel_id=1, source_target_pairs={{0,1},{1,0},{2,3},{3,2},{4,5},{5,4},{6,7},{7,6}} | collective-permute-start | bytes 3538952 | tf_op jit(solution)/shard_map/ppermute | solution.py:24
  171.3 26.0 %collective-permute-start.9 = (bf16[512,2304]{1,0:T(8,128)(2,1)}, bf16[512,2304]{1,0:T(8,128)(2,1)}, u32[]{:S(2)}, u32[]{:S(2)}) collective-permute-start(bf16[512,2304]{1,0:T(8,128)(2,1)} %get-tuple-element.36), channel_id=1, source_target_pairs={{0,1},{1,0},{2,3},{3,2},{4,5},{5,4},{6,7},{7,6}} | collective-permute-start | bytes 7077896 | tf_op jit(solution)/shard_map/ppermute | solution.py:24
  251.7 61.5 %collective-permute-start.10 = (bf16[512,2304]{1,0:T(8,128)(2,1)}, bf16[512,2304]{1,0:T(8,128)(2,1)}, u32[]{:S(2)}, u32[]{:S(2)}) collective-permute-start(bf16[512,2304]{1,0:T(8,128)(2,1)} %get-tuple-element.41), channel_id=1, source_target_pairs={{0,1},{1,0},{2,3},{3,2},{4,5},{5,4},{6,7},{7,6}} | collective-permute-start | bytes 7077896 | tf_op jit(solution)/shard_map/ppermute | solution.py:24
  259.7 29.2 %collective-permute-start.11 = (bf16[256,2304]{1,0:T(8,128)(2,1)}, bf16[256,2304]{1,0:T(8,128)(2,1)}, u32[]{:S(2)}, u32[]{:S(2)}) collective-permute-start(bf16[256,2304]{1,0:T(8,128)(2,1)} %get-tuple-element.37), channel_id=1, source_target_pairs={{0,2},{1,3},{2,0},{3,1},{4,6},{5,7},{6,4},{7,5}} | collective-permute-start | bytes 3538952 | tf_op jit(solution)/shard_map/ppermute | solution.py:24
  259.7 53.5 %collective-permute-start.12 = (bf16[256,2304]{1,0:T(8,128)(2,1)}, bf16[256,2304]{1,0:T(8,128)(2,1)}, u32[]{:S(2)}, u32[]{:S(2)}) collective-permute-start(bf16[256,2304]{1,0:T(8,128)(2,1)} %get-tuple-element.38), channel_id=1, source_target_pairs={{0,2},{1,3},{2,0},{3,1},{4,6},{5,7},{6,4},{7,5}} | collective-permute-start | bytes 3538952 | tf_op jit(solution)/shard_map/ppermute | solution.py:24
